TPU v7x, 32 devices: a whole 2x2x4 slice. The times are simulated.
32 devices in a mesh: seq: 4 (over y, core), span: 8 (over z, x).
Axes of the slice: x: 2, y: 2, z: 4, core: 2. Of those that a mesh axis runs over, the one named last changes fastest.
Arguments:
- queries: bfloat16 [8, 512, 1536], P('span', 'seq'), may hold values from -6 to 6
- key_head_matrix: bfloat16 [8, 512, 512], P('span', 'seq'), may hold values from -6 to 6
- value_head_matrix: bfloat16 [8, 512, 512], P('span', 'seq'), may hold values from -6 to 6
- attn_output: bfloat16 [8, 512, 1536], P('span', 'seq'), may hold values from -6 to 6
- out_grad: bfloat16 [8, 512, 1536], P('span', 'seq'), may hold values from -6 to 6
Outputs:
- query_grad: bfloat16 [8, 512, 1536], P('span', 'seq')
- key_grad: bfloat16 [8, 512, 512], P('span', 'seq')
- value_grad: bfloat16 [8, 512, 512], P('span', 'seq')
All inputs are finite; a program needn't handle non-finite values.
Results may differ from a plain program's by a relative error of at most 0.005.
Values may be sent and summed in bfloat16 or wider, within the bound.
A program may use at most 64 MiB of HBM per device.

v0:
```python
import functools
import math

import jax
import jax.numpy as jnp
from jax import lax
from jax.experimental import pallas as pl
from jax.experimental.pallas import tpu as pltpu
from jax.sharding import PartitionSpec as P

HEAD_WIDTH = 64
QUERY_PER_KEY = 3
NEG_LARGE = -1e30
MESH = pl.DeviceIdType.MESH
LOG2E = math.log2(math.e)
SCORE_BYTES = 34 * 2**20


def place(group):
    seq_count = lax.axis_size("seq")
    span = lax.axis_index("span")
    layers = lax.axis_size("span") // group
    mine = lax.rem(span, group) * seq_count + lax.axis_index("seq")
    return span // group, mine, layers, group * seq_count


def device_of(layer, spot, group):
    seq_count = lax.axis_size("seq")
    return {"seq": lax.rem(spot, seq_count), "span": layer * group + spot // seq_count}


def given_heads(layer, layers):
    surplus = QUERY_PER_KEY * 2 * (2 * layer + 1 - layers)
    count = (jnp.maximum(surplus, 0) + layer + 1) // (2 * layer + 2)
    return jnp.where(surplus > 0, jnp.minimum(count, QUERY_PER_KEY), 0)


def score_blocks(layers, rows, block):
    most = 0
    per = rows // block
    for layer in range(layers):
        mirror = layers - 1 - layer
        counts = []
        for one in (layer, mirror):
            surplus = QUERY_PER_KEY * 2 * (2 * one + 1 - layers)
            count = min((max(surplus, 0) + one + 1) // (2 * one + 2), QUERY_PER_KEY)
            counts.append(count if surplus > 0 else 0)
        own = QUERY_PER_KEY * (layer * per + per // 2) + (QUERY_PER_KEY - counts[0]) * (layer + 1) * per
        most = max(most, own + counts[1] * (mirror + 1) * per)
    return most


def top_layer(layer, layers):
    mirror = layers - 1 - layer
    return jnp.where(given_heads(mirror, layers) > 0, mirror, layer)


def dot(a, b, contract):
    return lax.dot_general(a, b, ((contract[:1], contract[1:]), ((), ())), preferred_element_type=jnp.float32)


def kernel(group, tq, tk, resident, qg_ref, kv_ref, dl_ref, dq_out, dkv_out,
           qg_in, kv_in, dl_in, s_ref, dl_row, q_pad, g_pad, m_ref, l_ref, dqt_ref, acc_ref, dq_ref, dkv_ref,
           q_send, q_recv, kv_send, kv_recv, dl_send, dl_recv,
           dq_send, dq_recv, ex_send, dkv_send, dkv_recv, q_local, dq_local, local_sem):
    layer, mine, layers, spots = place(group)
    heads = QUERY_PER_KEY
    half = spots // 2
    tokens = qg_ref.shape[2]
    rows = spots * tokens
    mirror = layers - 1 - layer
    given = given_heads(layer, layers)
    taken = given_heads(mirror, layers)
    top = top_layer(layer, layers)
    scaling = 1.0 / math.sqrt(HEAD_WIDTH)
    factor = scaling * LOG2E

    def spot_at(offset):
        return lax.rem(mine + offset, spots)

    def spot_from(offset):
        return lax.rem(mine + spots - offset, spots)

    def remote(source, target, send, recv, to_layer, spot):
        return pltpu.make_async_remote_copy(
            src_ref=source, dst_ref=target, send_sem=send, recv_sem=recv,
            device_id=device_of(to_layer, spot, group), device_id_type=MESH)

    def is_given(spot, h):
        return jnp.logical_and(spot >= half, h >= heads - given)

    def q_copy(h, offset):
        away = is_given(mine, h)
        slot = jnp.where(away, heads + h + given, (mine // half) * heads + h)
        spot = spot_at(offset)
        return remote(qg_ref.at[spot, h], qg_in.at[slot, lax.rem(mine, half)],
                      q_send.at[h, offset], q_recv.at[jnp.where(away, 1, 0), h, offset],
                      jnp.where(away, mirror, layer), spot)

    def q_arrival(kind, h, offset):
        return remote(qg_ref.at[0, h], qg_in.at[0, 0], q_send.at[h, offset], q_recv.at[kind, h, offset], mirror, mine)

    def q_own(h):
        return pltpu.make_async_copy(
            qg_ref.at[mine, h], qg_in.at[(mine // half) * heads + h, lax.rem(mine, half)], q_local.at[h])

    def dl_copy(kind, offset):
        spot = spot_at(offset)
        return remote(dl_ref.at[spot], dl_in.at[kind, mine], dl_send.at[kind, offset], dl_recv.at[kind, offset],
                      layer if kind == 0 else mirror, spot)

    def kv_copy(to_layer, offset):
        spot = spot_at(offset)
        return remote(kv_ref.at[spot], kv_in.at[layer, mine], kv_send.at[to_layer, offset],
                      kv_recv.at[layer, offset], to_layer, spot)

    def kv_arrival(from_layer, offset):
        return remote(kv_ref.at[0], kv_in.at[0, 0], kv_send.at[0, offset], kv_recv.at[from_layer, offset],
                      layer, mine)

    def dq_copy(slot_base, h, offset):
        spot = spot_at(offset)
        return remote(dq_ref.at[(spot // half) * heads + h, lax.rem(spot, half)], dq_out.at[mine, h],
                      dq_send.at[h, offset], dq_recv.at[h, offset], layer, spot)

    def dq_own(h):
        return pltpu.make_async_copy(
            dq_ref.at[(mine // half) * heads + h, lax.rem(mine, half)], dq_out.at[mine, h], dq_local.at[h])

    def dq_extra(k, u):
        spot = half + u
        h = heads - taken + k
        return remote(dq_ref.at[2 * heads + k, u], dq_out.at[mine, h], ex_send.at[k, u],
                      dq_recv.at[h, lax.rem(spot + spots - mine, spots)], mirror, spot)

    def dkv_copy(to_layer, offset):
        spot = spot_at(offset)
        return remote(dkv_ref.at[to_layer, spot], dkv_out.at[layer, mine], dkv_send.at[to_layer, offset],
                      dkv_recv.at[layer, offset], to_layer, spot)

    def dkv_arrival(from_layer, offset):
        return remote(dkv_ref.at[0, 0], dkv_out.at[0, 0], dkv_send.at[0, offset],
                      dkv_recv.at[from_layer, offset], layer, mine)

    kv_own = pltpu.make_async_copy(kv_ref.at[mine], kv_in.at[layer, mine], local_sem.at[0])
    dl_own = pltpu.make_async_copy(dl_ref.at[mine], dl_in.at[0, mine], local_sem.at[1])
    dkv_own = pltpu.make_async_copy(dkv_ref.at[layer, mine], dkv_out.at[layer, mine], local_sem.at[2])
    gives_now = jnp.logical_and(mine >= half, given > 0)

    for h in range(heads):
        @pl.when(is_given(mine, h))
        def _():
            for offset in range(spots):
                q_copy(h, offset).start()

    @pl.when(gives_now)
    def _():
        for offset in range(spots):
            dl_copy(1, offset).start()

    for offset in range(spots):
        for step in range(layers - 1, 0, -1):
            other = lax.rem(layer + step, layers)

            @pl.when(top_layer(other, layers) >= layer)
            def _():
                kv_copy(other, offset).start()

        if offset:
            kv_copy(layer, offset).start()
            dl_copy(0, offset).start()
        else:
            kv_own.start()
            dl_own.start()
        for h in range(heads):
            @pl.when(jnp.logical_not(is_given(mine, h)))
            def _():
                if offset:
                    q_copy(h, offset).start()
                else:
                    q_own(h).start()

    blocks_here = rows // tk

    def clear(j, _):
        acc_ref[pl.ds(pl.multiple_of(j * tk, tk), tk), :] = jnp.zeros((tk, 2 * HEAD_WIDTH), jnp.float32)
        return 0

    lax.fori_loop(0, (top + 1) * blocks_here, clear, 0)

    kv_own.wait()
    dl_own.wait()
    for offset in range(1, spots):
        dl_copy(0, offset).wait_recv()
        kv_arrival(layer, offset).wait_recv()
    for h in range(heads):
        for offset in range(1, spots):
            @pl.when(jnp.logical_not(is_given(spot_from(offset), h)))
            def _():
                q_arrival(0, h, offset).wait_recv()

        @pl.when(jnp.logical_not(is_given(mine, h)))
        def _():
            q_own(h).wait()

    subs = half * tokens // tq
    pieces = tq // tokens
    lane = lax.broadcasted_iota(jnp.int32, (1, 2 * HEAD_WIDTH), 1)
    own_jobs = (2 * heads - given) * subs
    jobs = (2 * heads - given + taken) * subs

    def job_place(i):
        slot = i // subs
        sub = lax.rem(i, subs)
        extra = slot >= 2 * heads
        q_layer = jnp.where(extra, mirror, layer)
        q_first = q_layer * rows + jnp.where(slot >= heads, half * tokens, 0) + sub * tq
        low_blocks = layer * blocks_here + blocks_here // 2
        high_blocks = (layer + 1) * blocks_here
        base = jnp.where(slot < heads, slot * low_blocks, heads * low_blocks + (slot - heads) * high_blocks)
        base = jnp.where(extra, heads * (low_blocks + high_blocks) + (slot - 2 * heads) * (mirror + 1) * blocks_here,
                         base)
        return slot, sub, extra, q_first, q_first // tk, base

    def prepare(i, _):
        slot, sub, extra, _, _, _ = job_place(i)
        head = jnp.where(extra, slot - heads - taken, lax.rem(slot, heads))
        both = qg_in[slot, pl.ds(sub * pieces, pieces)].reshape(tq, 2 * HEAD_WIDTH)
        q_pad[i] = jnp.where(lane < HEAD_WIDTH, both, jnp.zeros_like(both))
        g_pad[i] = jnp.where(lane < HEAD_WIDTH, jnp.zeros_like(both), both)
        for piece in range(pieces):
            spot = jnp.where(slot >= heads, half, 0) + sub * pieces + piece
            dl_row[i, :, piece * tokens:(piece + 1) * tokens] = (
                dl_in[jnp.where(extra, 1, 0), spot, pl.ds(head, 1), :])
        dqt_ref[i] = jnp.zeros((HEAD_WIDTH, tq), jnp.float32)
        m_ref[i] = jnp.full((1, tq), NEG_LARGE, jnp.float32)
        l_ref[i] = jnp.zeros((1, tq), jnp.float32)
        return 0

    def kv_block(j):
        per = tk // tokens
        at = kv_in[j // blocks_here, pl.ds(lax.rem(j, blocks_here) * per, per)]
        return at.reshape(tk, 2 * HEAD_WIDTH)

    def hide(s, j, q_first):
        k_pos = j * tk + lax.broadcasted_iota(jnp.int32, (tk, tq), 0)
        q_pos = q_first + lax.broadcasted_iota(jnp.int32, (tk, tq), 1)
        return jnp.where(k_pos <= q_pos, s, NEG_LARGE)

    def layer_stats(l, low, high):
        def one_job(i, _):
            _, _, _, q_first, last, base = job_place(i)

            def block(j, masked):
                s = dot(kv_block(j), q_pad[i], (1, 1))
                if masked:
                    s = hide(s, j, q_first)
                if resident:
                    s_ref[base + j] = s
                m_old = m_ref[i]
                m_new = jnp.maximum(m_old, jnp.max(s, axis=0, keepdims=True))
                e = jnp.exp2((s - m_new) * factor)
                l_ref[i] = l_ref[i] * jnp.exp2((m_old - m_new) * factor) + jnp.sum(e, axis=0, keepdims=True)
                m_ref[i] = m_new
                return 0

            end = (l + 1) * blocks_here
            lax.fori_loop(l * blocks_here, jnp.minimum(end, last), lambda j, _: block(j, False), 0)

            @pl.when(last < end)
            def _():
                @pl.when(last >= l * blocks_here)
                def _():
                    block(last, True)
            return 0

        lax.fori_loop(low, high, one_job, 0)

    def wait_layer(l):
        for offset in range(spots):
            kv_arrival(l, offset).wait_recv()

    lax.fori_loop(0, own_jobs, prepare, 0)

    def own_stats(t, _):
        l = layer - t

        @pl.when(t > 0)
        def _():
            wait_layer(l)

        layer_stats(l, 0, own_jobs)
        return 0

    lax.fori_loop(0, layer + 1, own_stats, 0)

    @pl.when(taken > 0)
    def _():
        for offset in range(spots):
            @pl.when(spot_from(offset) >= half)
            def _():
                dl_copy(1, offset).wait_recv()
                for h in range(heads):
                    @pl.when(h >= heads - taken)
                    def _():
                        q_arrival(1, h, offset).wait_recv()

        lax.fori_loop(own_jobs, jobs, prepare, 0)

        def extra_stats(l, _):
            @pl.when(l > layer)
            def _():
                wait_layer(l)

            layer_stats(l, own_jobs, jobs)
            return 0

        lax.fori_loop(0, top + 1, extra_stats, 0)

    def norms(i, _):
        m_ref[i] = m_ref[i] * factor + jnp.log2(l_ref[i])
        return 0

    lax.fori_loop(0, jobs, norms, 0)

    def layer_grads(t, _):
        above = top - layer
        l = jnp.where(t < above, top - t, t - above)

        def one_job(i, _):
            slot, sub, extra, q_first, last, base = job_place(i)

            def grads(j, _):
                at = pl.ds(pl.multiple_of(j * tk, tk), tk)
                kv = kv_block(j)
                if resident:
                    s = s_ref[base + j]
                else:
                    s = hide(dot(kv, q_pad[i], (1, 1)), j, q_first)
                p = jnp.exp2(s * factor - m_ref[i])
                dp = dot(kv, g_pad[i], (1, 1))
                ds = (p * (dp - dl_row[i])).astype(jnp.bfloat16)
                acc_ref[at, :] += dot(ds, q_pad[i], (1, 0)) + dot(p.astype(jnp.bfloat16), g_pad[i], (1, 0))
                dqt_ref[i] += dot(kv[:, :HEAD_WIDTH].T, ds, (1, 0))
                return 0

            lax.fori_loop(l * blocks_here, jnp.minimum((l + 1) * blocks_here, last + 1), grads, 0)

            @pl.when(t == top)
            def _():
                for piece in range(pieces):
                    part = dqt_ref[i, :, piece * tokens:(piece + 1) * tokens] * scaling
                    dq_ref[slot, sub * pieces + piece] = part.astype(jnp.bfloat16)

                @pl.when(jnp.logical_and(sub == subs - 1, extra))
                def _():
                    for u in range(half):
                        dq_extra(slot - 2 * heads, u).start()

                @pl.when(jnp.logical_and(sub == subs - 1, jnp.logical_not(extra)))
                def _():
                    for offset in range(spots):
                        @pl.when(spot_at(offset) // half == slot // heads)
                        def _():
                            if offset:
                                dq_copy(0, lax.rem(slot, heads), offset).start()
                            else:
                                dq_own(lax.rem(slot, heads)).start()
            return 0

        lax.fori_loop(0, jobs, one_job, 0)

        def finish(spot, _):
            at = pl.ds(pl.multiple_of(l * rows + spot * tokens, tokens), tokens)
            part = acc_ref[at, :] * jnp.where(lane < HEAD_WIDTH, scaling, 1.0)
            dkv_ref[l, spot] = part.astype(jnp.bfloat16)
            return 0

        lax.fori_loop(0, spots, finish, 0)
        for offset in range(1, spots):
            dkv_copy(l, offset).start()

        @pl.when(l == layer)
        def _():
            dkv_own.start()

        @pl.when(l != layer)
        def _():
            dkv_copy(l, 0).start()
        return 0

    lax.fori_loop(0, top + 1, layer_grads, 0)

    for h in range(heads):
        for offset in range(1, spots):
            q_copy(h, offset).wait_send()

            @pl.when(jnp.logical_not(is_given(spot_at(offset), h)))
            def _():
                dq_copy(0, h, offset).wait_send()
            dq_copy(0, h, offset).wait_recv()

        @pl.when(is_given(mine, h))
        def _():
            q_copy(h, 0).wait_send()
            dq_copy(0, h, 0).wait_recv()

        @pl.when(jnp.logical_not(is_given(mine, h)))
        def _():
            dq_own(h).wait()

        @pl.when(h < taken)
        def _():
            for u in range(half):
                dq_extra(h, u).wait_send()
    for offset in range(1, spots):
        dl_copy(0, offset).wait_send()

    @pl.when(gives_now)
    def _():
        for offset in range(spots):
            dl_copy(1, offset).wait_send()

    dkv_own.wait()
    for other in range(layers):
        away = other != layer

        @pl.when(top_layer(other, layers) >= layer)
        def _():
            for offset in range(1, spots):
                kv_copy(other, offset).wait_send()
                dkv_arrival(other, offset).wait_recv()

            @pl.when(away)
            def _():
                kv_copy(other, 0).wait_send()
                dkv_arrival(other, 0).wait_recv()

        @pl.when(other <= top)
        def _():
            for offset in range(1, spots):
                dkv_copy(other, offset).wait_send()

            @pl.when(away)
            def _():
                dkv_copy(other, 0).wait_send()


def vmem(count):
    return [pl.BlockSpec(memory_space=pltpu.VMEM)] * count


def per_device(queries, key_head_matrix, value_head_matrix, attn_output, out_grad):
    seq_count = lax.axis_size("seq")
    tokens = queries.shape[1]
    group = key_head_matrix.shape[2] // (HEAD_WIDTH * seq_count)
    layers = lax.axis_size("span") // group
    spots = group * seq_count
    heads = QUERY_PER_KEY
    half = spots // 2
    pair = 2 * HEAD_WIDTH
    rows = spots * tokens

    def by_spot(source, count):
        split = source.reshape(tokens, seq_count, group, count, HEAD_WIDTH)
        return jnp.transpose(split, (2, 1, 3, 0, 4)).reshape(spots, count, tokens, HEAD_WIDTH)

    qg = jnp.concatenate([by_spot(queries[0], heads), by_spot(out_grad[0], heads)], axis=3)
    kv = jnp.concatenate([by_spot(key_head_matrix[0], 1), by_spot(value_head_matrix[0], 1)], axis=3)[:, 0]
    product = out_grad[0].astype(jnp.float32) * attn_output[0].astype(jnp.float32)
    delta = jnp.sum(product.reshape(tokens, seq_count, group, heads, HEAD_WIDTH), axis=4)
    delta = jnp.transpose(delta, (2, 1, 3, 0)).reshape(spots, heads, tokens)
    delta = jnp.pad(delta, ((0, 0), (0, 8 - heads), (0, 0)))

    tk = math.gcd(rows, 512)
    tq = half * tokens
    while tq > tk or tk % tq:
        tq //= 2
    count = score_blocks(layers, rows, tk)
    resident = tq == tk == half * tokens and count * tk * tq * 4 <= SCORE_BYTES
    slots = 3 * heads
    all_jobs = slots * half * tokens // tq
    dma = pltpu.SemaphoreType.DMA
    dq_all, dkv_all = pl.pallas_call(
        functools.partial(kernel, group, tq, tk, resident),
        out_shape=(
            jax.ShapeDtypeStruct((spots, heads, HEAD_WIDTH, tokens), jnp.bfloat16),
            jax.ShapeDtypeStruct((layers, spots, tokens, pair), jnp.bfloat16),
        ),
        in_specs=vmem(3),
        out_specs=tuple(vmem(2)),
        scratch_shapes=[
            pltpu.VMEM((3 * heads, half, tokens, pair), jnp.bfloat16),
            pltpu.VMEM((layers, spots, tokens, pair), jnp.bfloat16),
            pltpu.VMEM((2, spots, 8, tokens), jnp.float32),
            pltpu.VMEM((count, tk, tq) if resident else (1, 8, tq), jnp.float32),
            pltpu.VMEM((all_jobs, 1, tq), jnp.float32),
            pltpu.VMEM((all_jobs, tq, pair), jnp.bfloat16),
            pltpu.VMEM((all_jobs, tq, pair), jnp.bfloat16),
            pltpu.VMEM((all_jobs, 1, tq), jnp.float32),
            pltpu.VMEM((all_jobs, 1, tq), jnp.float32),
            pltpu.VMEM((all_jobs, HEAD_WIDTH, tq), jnp.float32),
            pltpu.VMEM((layers * rows, pair), jnp.float32),
            pltpu.VMEM((3 * heads, half, HEAD_WIDTH, tokens), jnp.bfloat16),
            pltpu.VMEM((layers, spots, tokens, pair), jnp.bfloat16),
            dma((heads, spots)),
            dma((2, heads, spots)),
            dma((layers, spots)),
            dma((layers, spots)),
            dma((2, spots)),
            dma((2, spots)),
            dma((heads, spots)),
            dma((heads, spots)),
            dma((heads, half)),
            dma((layers, spots)),
            dma((layers, spots)),
            dma((heads,)),
            dma((heads,)),
            dma((3,)),
        ],
        compiler_params=pltpu.CompilerParams(has_side_effects=True, vmem_limit_bytes=60 * 2**20),
        name="attention_grads",
    )(qg, kv, delta)

    dq = dq_all.reshape(group, seq_count, heads * HEAD_WIDTH, tokens)
    dq = jnp.transpose(dq, (3, 1, 0, 2)).reshape(1, tokens, -1)

    def by_token(source):
        split = source.reshape(group, seq_count, tokens, source.shape[-1])
        return jnp.transpose(split, (2, 1, 0, 3)).reshape(1, tokens, -1)

    layer = lax.axis_index("span") // group
    senders = lax.broadcasted_iota(jnp.int32, (layers, 1, 1, 1), 0)
    came = top_layer(senders, layers) >= layer
    kv_sum = jnp.sum(jnp.where(came, dkv_all.astype(jnp.float32), 0.0), axis=0).astype(jnp.bfloat16)
    return dq, by_token(kv_sum[..., :HEAD_WIDTH]), by_token(kv_sum[..., HEAD_WIDTH:])


def solution(mesh):
    spec = P("span", "seq", None)
    return jax.shard_map(
        per_device, mesh=mesh, in_specs=(spec,) * 5, out_specs=(spec,) * 3, check_vma=False
    )
```

profile of v0, /device:TPU:0, one launch (start us, length us, event | category | flops | bytes accessed | tf_op | source)
XLA Modules:
  0.0 91.4 jit_solution(8464060309805732009)
XLA Ops:
  0.6 0.1 fusion.4
  0.8 0.0 copy-start.1
  0.8 1.1 %copy.32 = bf16[1,128,512]{1,2,0:T(8,128)(2,1)S(1)} copy(bf16[1,128,512]{2,1,0:T(8,128)(2,1)} %param.6) | data formatting | bytes 262144 | tf_op args[1]
  1.9 0.2 copy.33
  2.1 1.0 %copy.34 = bf16[1,128,512]{1,2,0:T(8,128)(2,1)S(1)} copy(bf16[1,128,512]{2,1,0:T(8,128)(2,1)} %param.7) | data formatting | bytes 262144 | tf_op args[2]
  3.1 0.0 copy-start.2
  3.1 0.2 copy.35
  3.3 0.9 maximum_bitcast_fusion.kv_ref
  4.1 0.0 copy-done.1
  4.2 0.2 copy.30
  4.4 0.0 copy-start.3
  4.4 0.0 copy-done.2
  4.4 0.2 copy.28
  4.6 0.4 copy.29
  5.0 0.4 copy-done.3
  5.4 0.2 copy.36
  5.6 0.2 fusion
  5.8 0.6 pad.4.dl_ref
  6.4 0.4 copy.31
  6.8 1.4 %pad_maximum_fusion.qg_ref = bf16[8,3,128,128]{3,2,1,0:T(8,128)(2,1)} fusion(bf16[8,3,128,64]{3,2,1,0:T(8,128)(2,1)S(1)} %bitcast.37, bf16[8,3,128,64]{3,2,1,0:T(8,128)(2,1)S(1)} %bitcast.36), kind=kLoop, calls=%fused_computation.1 | loop fusion | flops 1572864 | bytes 1572864 | tf_op jit(solution)/shard_map/concatenate | solution.py:468
  8.2 78.9 %attention_grads.1 = (bf16[8,3,64,128]{3,2,1,0:T(8,128)(2,1)}, bf16[4,8,128,128]{3,2,1,0:T(8,128)(2,1)}) custom-call(bf16[8,3,128,128]{3,2,1,0:T(8,128)(2,1)} %pad_maximum_fusion.qg_ref, bf16[8,128,128]{2,1,0:T(8,128)(2,1)} %maximum_bitcast_fusion.kv_ref, f32[8,8,128]{2,1,0:T(8,128)} %pad.4.dl_ref), custom_call_target="tpu_custom_call" | custom-call | tf_op jit(solution)/shard_map/attention_grads/pallas_call | solution.py:484
  87.1 0.0 copy-start
  87.1 1.1 %copy.38 = bf16[2,4,192,128]{3,2,0,1:T(8,128)(2,1)S(1)} copy(bf16[2,4,192,128]{3,2,1,0:T(8,128)(2,1)} %bitcast.49) | data formatting | bytes 786432 | tf_op jit(solution)/shard_map/reshape | solution.py:525
  88.2 0.9 %copy.43 = bf16[1,128,1536]{2,1,0:T(8,128)(2,1)} copy(bf16[1,128,1536]{1,2,0:T(8,128)(2,1)S(1)} %bitcast.38) | data formatting | bytes 786432
  89.1 0.0 copy-done
  89.1 0.3 select_reduce_fusion
  89.4 0.1 fusion.5
  89.5 0.1 copy.42
  89.7 0.8 copy.45
  90.4 0.1 copy.40
  90.6 0.8 copy.44
  (1 shorter events, 0.0 us)
Async XLA Ops:
  0.8 3.4 %copy-start.1 = (bf16[1,128,1536]{2,1,0:T(8,128)(2,1)S(1)}, bf16[1,128,1536]{2,1,0:T(8,128)(2,1)}, u32[]{:S(2)}) copy-start(bf16[1,128,1536]{2,1,0:T(8,128)(2,1)} %param.9) | copy-start | bytes 1179652
  3.1 1.3 %copy-start.2 = (bf16[1,128,1536]{2,1,0:T(8,128)(2,1)S(1)}, bf16[1,128,1536]{2,1,0:T(8,128)(2,1)}, u32[]{:S(2)}) copy-start(bf16[1,128,1536]{2,1,0:T(8,128)(2,1)} %param.5) | copy-start | bytes 1179652
  4.4 1.0 %copy-start.3 = (bf16[1,128,1536]{2,1,0:T(8,128)(2,1)S(1)}, bf16[1,128,1536]{2,1,0:T(8,128)(2,1)}, u32[]{:S(2)}) copy-start(bf16[1,128,1536]{2,1,0:T(8,128)(2,1)} %param.8) | copy-start | bytes 1179652
  87.1 2.1 %copy-start = (bf16[4,8,128,128]{3,2,1,0:T(8,128)(2,1)S(1)}, bf16[4,8,128,128]{3,2,1,0:T(8,128)(2,1)}, u32[]{:S(2)}) copy-start(bf16[4,8,128,128]{3,2,1,0:T(8,128)(2,1)} %get-tuple-element.6) | copy-start | bytes 3145732
where the time goes:
time: 92.7 us; the launch traced here: 91.4 us
  Pallas kernels  78.9 us (85%)
  local copies, waits for them, and re-layouts  8.89 us (10%)
  other arithmetic  2.78 us (3%)
    pallas_call x1, Pallas kernels, per_device(): pl.pallas_call(functools.partial(kernel, group, tq, tk, resident), out_sh...  78.9 us
    unnamed x16, local copies, waits for them, and re-layouts  5.6 us

commit v1 on v0

v1 whole, which is shorter than its diff:
```python
import functools
import math

import jax
import jax.numpy as jnp
from jax import lax
from jax.experimental import pallas as pl
from jax.experimental.pallas import tpu as pltpu
from jax.sharding import PartitionSpec as P

HEAD_WIDTH = 64
PAIR = 2 * HEAD_WIDTH
QUERY_PER_KEY = 3
NEG_LARGE = -1e30
MESH = pl.DeviceIdType.MESH
LOG2E = math.log2(math.e)
SCORE_BYTES = 26 * 2**20


def dot(a, b, contract):
    return lax.dot_general(a, b, ((contract[:1], contract[1:]), ((), ())), preferred_element_type=jnp.float32)


def kernel(kv_heads, resident, q_ref, k_ref, v_ref, o_ref, g_ref, dq_out, dk_out, dv_out,
           qg_send, kv_send, dl_send, qg_in, kv_in, dl_in, q_pad, g_pad, dl_row, s_ref, m_ref, l_ref, dqt_ref,
           acc_ref, dq_send, dq_in, part_ref, red_in, fin_ref, dkv_in,
           qg_s, qg_r, kv_s, kv_r, dl_s, dl_r, side_s, hand_s, dq_s, dq_r, red_s, red_r, fin_s, fin_r):
    seq_count = lax.axis_size("seq")
    seq = lax.axis_index("seq")
    span = lax.axis_index("span")
    heads = QUERY_PER_KEY
    spread = lax.axis_size("span") // kv_heads
    splits = spread * seq_count
    tokens = q_ref.shape[1]
    per = kv_heads // 2
    chunk = per * tokens
    top = 2 * splits - 1
    me = span * seq_count + seq
    my_head = span // spread
    my_split = lax.rem(span, spread) * seq_count + seq
    scaling = 1.0 / math.sqrt(HEAD_WIDTH)
    factor = scaling * LOG2E

    def rank_of(split):
        return 2 * lax.rem(split, splits // 2) + split // (splits // 2)

    def split_of(rank):
        return lax.rem(rank, 2) * (splits // 2) + rank // 2

    my_rank = rank_of(my_split)
    my_chunk = me // per
    my_kind = jnp.where(my_chunk < splits, 0, 1)
    my_sub = lax.rem(me, per)
    q_split = split_of(jnp.where(my_chunk < splits, my_chunk, top - my_chunk))

    def chunk_of(kind):
        return top - my_rank if kind else my_rank

    def member(head, split):
        return {"seq": lax.rem(split, seq_count), "span": head * spread + split // seq_count}

    def source(piece):
        return {"seq": lax.rem(piece, seq_count), "span": piece // seq_count}

    def remote(src, dst, send, recv, device):
        return pltpu.make_async_remote_copy(src_ref=src, dst_ref=dst, send_sem=send, recv_sem=recv,
                                            device_id=device, device_id_type=MESH)

    def other(mine, fn_other, fn_mine):
        @pl.when(mine)
        def _():
            fn_mine()

        @pl.when(jnp.logical_not(mine))
        def _():
            fn_other()

    def qg_copy(h, j):
        return remote(qg_send.at[h, j], qg_in.at[my_kind, j, my_sub], qg_s.at[h, j], qg_r.at[my_kind, j, my_sub],
                      member(h, q_split))

    def qg_own(h, j):
        return pltpu.make_async_copy(qg_send.at[h, j], qg_in.at[my_kind, j, my_sub], qg_s.at[h, j])

    def dl_copy(h):
        return remote(dl_send.at[h], dl_in.at[my_kind, my_sub], dl_s.at[h], dl_r.at[my_kind, my_sub],
                      member(h, q_split))

    def dl_own(h):
        return pltpu.make_async_copy(dl_send.at[h], dl_in.at[my_kind, my_sub], dl_s.at[h])

    def q_mine(h):
        return jnp.logical_and(h == my_head, q_split == my_split)

    def kv_copy(h):
        return remote(kv_send.at[h], kv_in.at[me], kv_s.at[h], kv_r.at[me], member(h, my_split))

    def kv_own(h):
        return pltpu.make_async_copy(kv_send.at[h], kv_in.at[me], kv_s.at[h])

    twin = my_split + 1 - 2 * lax.rem(my_split, 2)

    def step_split(k):
        return lax.rem(my_split + 2 * k, splits)

    def hand_copy(i, k):
        piece = i * splits + my_split
        return remote(kv_in.at[piece], kv_in.at[piece], hand_s.at[k, i], kv_r.at[piece],
                      member(my_head, step_split(k)))

    def twin_copy(i, k):
        piece = i * splits + step_split(k)
        return remote(kv_in.at[piece], kv_in.at[piece], side_s.at[k, i], kv_r.at[piece], member(my_head, twin))

    def kv_wait(piece):
        remote(kv_in.at[piece], kv_in.at[piece], kv_s.at[0], kv_r.at[piece], member(my_head, twin)).wait_recv()

    def dq_copy(kind, j, sub):
        piece = chunk_of(kind) * per + sub
        return remote(dq_send.at[kind, j, sub], dq_in.at[my_head, j], dq_s.at[kind, j, sub], dq_r.at[my_head, j],
                      source(piece))

    def dq_own(kind, j, sub):
        return pltpu.make_async_copy(dq_send.at[kind, j, sub], dq_in.at[my_head, j], dq_s.at[kind, j, sub])

    def red_copy(c, sub):
        piece = c * per + sub
        to = lax.rem(piece, splits)
        return remote(part_ref.at[piece], red_in.at[my_split, piece // splits], red_s.at[piece],
                      red_r.at[my_split, piece // splits], member(my_head, to))

    def fin_copy(i):
        return remote(fin_ref.at[i], dkv_in.at[my_head], fin_s.at[i], fin_r.at[my_head],
                      source(i * splits + my_split))

    def fin_own(i):
        return pltpu.make_async_copy(fin_ref.at[i], dkv_in.at[my_head], fin_s.at[i])

    for h in range(kv_heads):
        at = slice(h * HEAD_WIDTH, (h + 1) * HEAD_WIDTH)
        kv_send[h] = jnp.concatenate([k_ref[0, :, at], v_ref[0, :, at]], axis=1)
    for h in range(kv_heads):
        other(h == my_head, lambda: kv_copy(h).start(), lambda: kv_own(h).start())
    for j in range(heads):
        for h in range(kv_heads):
            one = h * heads + j
            at = slice(one * HEAD_WIDTH, (one + 1) * HEAD_WIDTH)
            qg_send[h, j] = jnp.concatenate([q_ref[0, :, at], g_ref[0, :, at]], axis=1)
        for h in range(kv_heads):
            other(q_mine(h), lambda: qg_copy(h, j).start(), lambda: qg_own(h, j).start())
    product = o_ref[0].astype(jnp.float32) * g_ref[0].astype(jnp.float32)
    high = product.astype(jnp.bfloat16)
    low = (product - high.astype(jnp.float32)).astype(jnp.bfloat16)
    wide = kv_heads * heads * HEAD_WIDTH
    row = lax.broadcasted_iota(jnp.int32, (kv_heads * 8, wide), 0)
    column = lax.broadcasted_iota(jnp.int32, (kv_heads * 8, wide), 1) // HEAD_WIDTH
    ones = jnp.where(row == (column // heads) * 8 + lax.rem(column, heads), 1.0, 0.0).astype(jnp.bfloat16)
    dl_send[...] = (dot(ones, high, (1, 1)) + dot(ones, low, (1, 1))).reshape(kv_heads, 8, tokens)
    for h in range(kv_heads):
        other(q_mine(h), lambda: dl_copy(h).start(), lambda: dl_own(h).start())

    def clear(b, _):
        acc_ref[b] = jnp.zeros((chunk, PAIR), jnp.float32)
        return 0

    lax.fori_loop(0, 2 * splits, clear, 0)

    def hand_on(i, _):
        piece = i * splits + my_split
        other(piece == me, lambda: kv_wait(piece), lambda: kv_own(my_head).wait())
        twin_copy(i, 0).start()
        for k in range(1, splits // 2):
            hand_copy(i, k).start()
        return 0

    lax.fori_loop(0, kv_heads, hand_on, 0)

    def pass_on(i, _):
        for k in range(1, splits // 2):
            kv_wait(i * splits + step_split(k))
            twin_copy(i, k).start()
        return 0

    lax.fori_loop(0, kv_heads, pass_on, 0)

    def twin_wait(i, _):
        for k in range(splits // 2):
            kv_wait(i * splits + lax.rem(twin + 2 * k, splits))
        return 0

    lax.fori_loop(0, kv_heads, twin_wait, 0)

    lane = lax.broadcasted_iota(jnp.int32, (1, PAIR), 1)

    def kv_block(b):
        return kv_in[pl.ds(b * per, per)].reshape(chunk, PAIR)

    def hide(s):
        k_pos = lax.broadcasted_iota(jnp.int32, (chunk, chunk), 0)
        q_pos = lax.broadcasted_iota(jnp.int32, (chunk, chunk), 1)
        return jnp.where(k_pos <= q_pos, s, NEG_LARGE)

    def scores(b, j, last):
        s = dot(kv_block(b), q_pad[j], (1, 1))
        return hide(s) if last else s

    for kind in range(2):
        c_q = chunk_of(kind)
        for j in range(heads):
            for sub in range(per):
                mine = c_q * per + sub == me
                landing = qg_in.at[kind, j, sub]
                other(mine,
                      lambda: remote(landing, landing, qg_s.at[0, j], qg_r.at[kind, j, sub],
                                     member(my_head, twin)).wait_recv(),
                      lambda: qg_own(my_head, j).wait())
                if j == 0:
                    small = dl_in.at[kind, sub]
                    other(mine,
                          lambda: remote(small, small, dl_s.at[0], dl_r.at[kind, sub],
                                         member(my_head, twin)).wait_recv(),
                          lambda: dl_own(my_head).wait())
            both = qg_in[kind, j].reshape(chunk, PAIR)
            q_pad[j] = jnp.where(lane < HEAD_WIDTH, both, jnp.zeros_like(both))
            g_pad[j] = jnp.where(lane < HEAD_WIDTH, jnp.zeros_like(both), both)
            for sub in range(per):
                dl_row[j, :, sub * tokens:(sub + 1) * tokens] = dl_in[kind, sub, pl.ds(j, 1), :]
            dqt_ref[j] = jnp.zeros((HEAD_WIDTH, chunk), jnp.float32)
            m_ref[j] = jnp.full((1, chunk), NEG_LARGE, jnp.float32)
            l_ref[j] = jnp.zeros((1, chunk), jnp.float32)

            def block(b, last):
                s = scores(b, j, last)
                if resident:
                    s_ref[b * heads + j] = s
                m_old = m_ref[j]
                m_new = jnp.maximum(m_old, jnp.max(s, axis=0, keepdims=True))
                e = jnp.exp2((s - m_new) * factor)
                l_ref[j] = l_ref[j] * jnp.exp2((m_old - m_new) * factor) + jnp.sum(e, axis=0, keepdims=True)
                m_ref[j] = m_new
                return 0

            lax.fori_loop(0, c_q, lambda b, _: block(b, False), 0)
            block(c_q, True)
            m_ref[j] = m_ref[j] * factor + jnp.log2(l_ref[j])

        def grads(b, last):
            kv = kv_block(b)
            total = jnp.zeros((chunk, PAIR), jnp.float32)
            for j in range(heads):
                s = s_ref[b * heads + j] if resident else scores(b, j, last)
                p = jnp.exp2(s * factor - m_ref[j])
                dp = dot(kv, g_pad[j], (1, 1))
                ds = (p * (dp - dl_row[j])).astype(jnp.bfloat16)
                total += dot(ds, q_pad[j], (1, 0)) + dot(p.astype(jnp.bfloat16), g_pad[j], (1, 0))
                dqt_ref[j] += dot(kv[:, :HEAD_WIDTH].T, ds, (1, 0))
            acc_ref[b] += total

        def hand_out(b):
            done = acc_ref[b] * jnp.where(lane < HEAD_WIDTH, scaling, 1.0)
            part_ref[pl.ds(b * per, per)] = done.astype(jnp.bfloat16).reshape(per, tokens, PAIR)
            for sub in range(per):
                @pl.when(lax.rem(b * per + sub, splits) != my_split)
                def _():
                    red_copy(b, sub).start()

        def reduce(b):
            for sub in range(per):
                piece = b * per + sub

                @pl.when(lax.rem(piece, splits) == my_split)
                def _():
                    i = piece // splits
                    at = pl.ds(pl.multiple_of(sub * tokens, tokens), tokens)

                    def add(f, _):
                        @pl.when(jnp.logical_and(f != my_split, top - rank_of(f) >= b))
                        def _():
                            landing = red_in.at[f, i]
                            remote(landing, landing, red_s.at[0], red_r.at[f, i], member(my_head, twin)).wait_recv()
                            acc_ref[b, at, :] += red_in[f, i].astype(jnp.float32) * jnp.where(
                                lane < HEAD_WIDTH, 1.0 / scaling, 1.0)
                        return 0

                    lax.fori_loop(0, splits, add, 0)
                    fin_ref[i] = (acc_ref[b, at, :] * jnp.where(lane < HEAD_WIDTH, scaling, 1.0)).astype(jnp.bfloat16)
                    other(piece == me, lambda: fin_copy(i).start(), lambda: fin_own(i).start())

        if kind == 0:
            lax.fori_loop(0, c_q, lambda b, _: (grads(b, False), 0)[1], 0)
            grads(c_q, True)
        else:
            def sweep(t, _):
                b = top - t

                @pl.when(b < c_q)
                def _():
                    grads(b, False)

                @pl.when(b == c_q)
                def _():
                    grads(b, True)

                @pl.when(b <= c_q)
                def _():
                    hand_out(b)

                @pl.when(t > 0)
                def _():
                    reduce(b + 1)
                return 0

            lax.fori_loop(0, top + 1, sweep, 0)

        for j in range(heads):
            for sub in range(per):
                part = dqt_ref[j, :, sub * tokens:(sub + 1) * tokens] * scaling
                dq_send[kind, j, sub] = part.astype(jnp.bfloat16)
        for j in range(heads):
            for sub in range(per):
                other(c_q * per + sub == me, lambda: dq_copy(kind, j, sub).start(),
                      lambda: dq_own(kind, j, sub).start())
    reduce(0)

    for h in range(kv_heads):
        for j in range(heads):
            mine = q_mine(h)
            landing = dq_in.at[h, j]
            other(mine,
                  lambda: remote(landing, landing, dq_s.at[0, j, 0], dq_r.at[h, j], member(my_head, twin)).wait_recv(),
                  lambda: dq_own(my_kind, j, my_sub).wait())
    dq_out[0] = dq_in[...].reshape(kv_heads * heads * HEAD_WIDTH, tokens).T
    for h in range(kv_heads):
        landing = dkv_in.at[h]
        other(h == my_head,
              lambda: remote(landing, landing, fin_s.at[0], fin_r.at[h], member(my_head, twin)).wait_recv(),
              lambda: fin_own(my_head).wait())
    for h in range(0, kv_heads, 2):
        at = slice(h * HEAD_WIDTH, (h + 2) * HEAD_WIDTH)
        dk_out[0, :, at] = jnp.concatenate([dkv_in[h, :, :HEAD_WIDTH], dkv_in[h + 1, :, :HEAD_WIDTH]], axis=1)
        dv_out[0, :, at] = jnp.concatenate([dkv_in[h, :, HEAD_WIDTH:], dkv_in[h + 1, :, HEAD_WIDTH:]], axis=1)

    for h in range(kv_heads):
        @pl.when(h != my_head)
        def _():
            kv_copy(h).wait_send()

        @pl.when(jnp.logical_not(q_mine(h)))
        def _():
            dl_copy(h).wait_send()
            for j in range(heads):
                qg_copy(h, j).wait_send()

    def sent(i, _):
        for k in range(splits // 2):
            twin_copy(i, k).wait_send()
            if k:
                hand_copy(i, k).wait_send()

        @pl.when(i != my_head)
        def _():
            fin_copy(i).wait_send()
        return 0

    lax.fori_loop(0, kv_heads, sent, 0)
    for kind in range(2):
        for j in range(heads):
            for sub in range(per):
                @pl.when(chunk_of(kind) * per + sub != me)
                def _():
                    dq_copy(kind, j, sub).wait_send()

    def red_sent(b, _):
        for sub in range(per):
            @pl.when(lax.rem(b * per + sub, splits) != my_split)
            def _():
                red_copy(b, sub).wait_send()
        return 0

    lax.fori_loop(0, chunk_of(1) + 1, red_sent, 0)


def vmem(count):
    return [pl.BlockSpec(memory_space=pltpu.VMEM)] * count


def per_device(queries, key_head_matrix, value_head_matrix, attn_output, out_grad):
    seq_count = lax.axis_size("seq")
    tokens = queries.shape[1]
    kv_heads = key_head_matrix.shape[2] // HEAD_WIDTH
    splits = lax.axis_size("span") // kv_heads * seq_count
    pieces = kv_heads * splits
    heads = QUERY_PER_KEY
    per = kv_heads // 2
    chunk = per * tokens
    count = heads * 2 * splits
    resident = count * chunk * chunk * 4 <= SCORE_BYTES
    dma = pltpu.SemaphoreType.DMA
    low, full = jnp.bfloat16, jnp.float32
    return pl.pallas_call(
        functools.partial(kernel, kv_heads, resident),
        out_shape=(
            jax.ShapeDtypeStruct(queries.shape, low),
            jax.ShapeDtypeStruct(key_head_matrix.shape, low),
            jax.ShapeDtypeStruct(value_head_matrix.shape, low),
        ),
        in_specs=vmem(5),
        out_specs=tuple(vmem(3)),
        scratch_shapes=[
            pltpu.VMEM((kv_heads, heads, tokens, PAIR), low),
            pltpu.VMEM((kv_heads, tokens, PAIR), low),
            pltpu.VMEM((kv_heads, 8, tokens), full),
            pltpu.VMEM((2, heads, per, tokens, PAIR), low),
            pltpu.VMEM((pieces, tokens, PAIR), low),
            pltpu.VMEM((2, per, 8, tokens), full),
            pltpu.VMEM((heads, chunk, PAIR), low),
            pltpu.VMEM((heads, chunk, PAIR), low),
            pltpu.VMEM((heads, 1, chunk), full),
            pltpu.VMEM((count, chunk, chunk) if resident else (1, 8, chunk), full),
            pltpu.VMEM((heads, 1, chunk), full),
            pltpu.VMEM((heads, 1, chunk), full),
            pltpu.VMEM((heads, HEAD_WIDTH, chunk), full),
            pltpu.VMEM((2 * splits, chunk, PAIR), full),
            pltpu.VMEM((2, heads, per, HEAD_WIDTH, tokens), low),
            pltpu.VMEM((kv_heads, heads, HEAD_WIDTH, tokens), low),
            pltpu.VMEM((pieces, tokens, PAIR), low),
            pltpu.VMEM((splits, kv_heads, tokens, PAIR), low),
            pltpu.VMEM((kv_heads, tokens, PAIR), low),
            pltpu.VMEM((kv_heads, tokens, PAIR), low),
            dma((kv_heads, heads)),
            dma((2, heads, per)),
            dma((kv_heads,)),
            dma((pieces,)),
            dma((kv_heads,)),
            dma((2, per)),
            dma((splits // 2, kv_heads)),
            dma((splits // 2, kv_heads)),
            dma((2, heads, per)),
            dma((kv_heads, heads)),
            dma((pieces,)),
            dma((splits, kv_heads)),
            dma((kv_heads,)),
            dma((kv_heads,)),
        ],
        compiler_params=pltpu.CompilerParams(has_side_effects=True, vmem_limit_bytes=60 * 2**20),
        name="attention_grads",
    )(queries, key_head_matrix, value_head_matrix, attn_output, out_grad)


def solution(mesh):
    spec = P("span", "seq", None)
    return jax.shard_map(
        per_device, mesh=mesh, in_specs=(spec,) * 5, out_specs=(spec,) * 3, check_vma=False
    )
```

time: 92.7 us -> 89.6 us (0.967)
  Pallas kernels: 78.9 us -> 84.7 us
  local copies, waits for them, and re-layouts: 8.89 us -> 3.41 us
  other arithmetic: 2.78 us -> 0 us
    pallas_call x1, Pallas kernels: 78.9 us -> 84.7 us  [per_device(): pl.pallas_call(functools.partial(kernel, kv_heads, resident), out_shape=(...]
    unnamed x16 -> x7, local copies, waits for them, and re-layouts: 5.6 us -> 3.41 us
    transpose x7 -> x0, local copies, waits for them, and re-layouts: 1.42 us -> none  [the longest x4 1.14 us: by_spot(): jnp.transpose(split, (2, 1, 3, 0, 4))]
    concatenate x1 -> x0, other arithmetic: 1.36 us -> none  [per_device(): jnp.concatenate([by_spot(queries[0], heads), by_spot(out_grad[0], heads)]...]
    reshape x1 -> x0, local copies, waits for them, and re-layouts: 1.11 us -> none  [per_device(): dq = dq_all.reshape(group, seq_count, heads * HEAD_WIDTH, tokens)]
where the time goes in v1:
time: 89.6 us; the launch traced here: 88.7 us
  Pallas kernels  84.7 us (95%)
  local copies, waits for them, and re-layouts  3.41 us (4%)
    pallas_call x1, Pallas kernels, per_device(): pl.pallas_call(functools.partial(kernel, kv_heads, resident), out_shape=(...  84.7 us
    unnamed x7, local copies, waits for them, and re-layouts  3.41 us

profile of v1, /device:TPU:0, one launch (start us, length us, event | category | flops | bytes accessed | tf_op | source)
XLA Modules:
  0.0 88.7 jit_solution(10581884988157763739)
XLA Ops:
  0.6 84.7 %attention_grads.1 = (bf16[1,128,1536]{2,1,0:T(8,128)(2,1)}, bf16[1,128,512]{2,1,0:T(8,128)(2,1)}, bf16[1,128,512]{2,1,0:T(8,128)(2,1)}) custom-call(bf16[1,128,1536]{2,1,0:T(8,128)(2,1)} %q_ref.1, bf16[1,128,512]{2,1,0:T(8,128)(2,1)} %k_ref.1, bf16[1,128,512]{2,1,0:T(8,128)(2,1)} %v_ref.1, bf16[1,128,1536]{2,1,0:T(8,128)(2,1)} %o_ref.1, ...), custom_call_target="tpu_custom_call" | custom-call | tf_op jit(solution)/shard_map/attention_grads/pallas_call | solution.py:400
  85.3 0.0 copy-start.1
  85.3 1.8 %copy.11 = bf16[1,128,1536]{2,1,0:T(8,128)(2,1)} copy(bf16[1,128,1536]{2,1,0:T(8,128)(2,1)} %get-tuple-element.6) | data formatting | bytes 786432
  87.1 0.0 copy-done.1
  87.1 0.0 copy-start
  87.1 0.7 copy.12
  87.8 0.3 copy-done
  88.1 0.7 copy.13
Async XLA Ops:
  85.3 1.8 %copy-start.1 = (bf16[1,128,512]{2,1,0:T(8,128)(2,1)S(1)}, bf16[1,128,512]{2,1,0:T(8,128)(2,1)}, u32[]{:S(2)}) copy-start(bf16[1,128,512]{2,1,0:T(8,128)(2,1)} %get-tuple-element.7) | copy-start | bytes 393220
  87.1 1.0 %copy-start = (bf16[1,128,512]{2,1,0:T(8,128)(2,1)S(1)}, bf16[1,128,512]{2,1,0:T(8,128)(2,1)}, u32[]{:S(2)}) copy-start(bf16[1,128,512]{2,1,0:T(8,128)(2,1)} %get-tuple-element.8) | copy-start | bytes 393220

commit v2 on v1

v2 whole, which is shorter than its diff:
```python
import functools
import math

import jax
import jax.numpy as jnp
from jax import lax
from jax.experimental import pallas as pl
from jax.experimental.pallas import tpu as pltpu
from jax.sharding import PartitionSpec as P

HEAD_WIDTH = 64
PAIR = 2 * HEAD_WIDTH
QUERY_PER_KEY = 3
NEG_LARGE = -1e30
MESH = pl.DeviceIdType.MESH
LOG2E = math.log2(math.e)
SCORE_BYTES = 30 * 2**20


def dot(a, b, contract):
    return lax.dot_general(a, b, ((contract[:1], contract[1:]), ((), ())), preferred_element_type=jnp.float32)


def kernel(kv_heads, resident, q_ref, k_ref, v_ref, o_ref, g_ref, dq_in, dkv_in,
           qg_send, kv_send, dl_send, qg_in, kv_in, dl_in, q_pad, g_pad, dl_row, s_ref, m_ref, l_ref, dqt_ref,
           acc_ref, dq_send, mate_in, part_ref, red_in, fin_ref,
           qg_s, qg_r, kv_s, kv_r, dl_s, dl_r, side_s, hand_s, dq_s, dq_r, mate_s, mate_r, red_s, red_r, fin_s, fin_r):
    seq_count = lax.axis_size("seq")
    seq = lax.axis_index("seq")
    span = lax.axis_index("span")
    heads = QUERY_PER_KEY
    spread = lax.axis_size("span") // kv_heads
    splits = spread * seq_count
    tokens = q_ref.shape[1]
    per = kv_heads // 2
    chunk = per * tokens
    top = 2 * splits - 1
    me = span * seq_count + seq
    my_head = span // spread
    my_split = lax.rem(span, spread) * seq_count + seq
    scaling = 1.0 / math.sqrt(HEAD_WIDTH)
    factor = scaling * LOG2E

    def rank_of(split):
        return 2 * lax.rem(split, splits // 2) + split // (splits // 2)

    def split_of(rank):
        return lax.rem(rank, 2) * (splits // 2) + rank // 2

    my_rank = rank_of(my_split)
    my_chunk = me // per
    my_kind = jnp.where(my_chunk < splits, 0, 1)
    my_sub = lax.rem(me, per)
    q_split = split_of(jnp.where(my_chunk < splits, my_chunk, top - my_chunk))

    def far(a, t):
        turned, unit = 0, 1
        while unit < kv_heads:
            turned += lax.rem(a // unit + t // unit, 2) * unit
            unit *= 2
        return turned

    def chunk_of(kind):
        return top - my_rank if kind else my_rank

    def member(head, split):
        return {"seq": lax.rem(split, seq_count), "span": head * spread + split // seq_count}

    def source(piece):
        return {"seq": lax.rem(piece, seq_count), "span": piece // seq_count}

    def remote(src, dst, send, recv, device):
        return pltpu.make_async_remote_copy(src_ref=src, dst_ref=dst, send_sem=send, recv_sem=recv,
                                            device_id=device, device_id_type=MESH)

    def other(mine, fn_other, fn_mine):
        @pl.when(mine)
        def _():
            fn_mine()

        @pl.when(jnp.logical_not(mine))
        def _():
            fn_other()

    def qg_copy(h, j):
        return remote(qg_send.at[h, j], qg_in.at[my_kind, j, my_sub], qg_s.at[h, j], qg_r.at[my_kind, j, my_sub],
                      member(h, q_split))

    def qg_own(h, j):
        return pltpu.make_async_copy(qg_send.at[h, j], qg_in.at[my_kind, j, my_sub], qg_s.at[h, j])

    def dl_copy(h):
        return remote(dl_send.at[h], dl_in.at[my_kind, my_sub], dl_s.at[h], dl_r.at[my_kind, my_sub],
                      member(h, q_split))

    def dl_own(h):
        return pltpu.make_async_copy(dl_send.at[h], dl_in.at[my_kind, my_sub], dl_s.at[h])

    def q_mine(h):
        return jnp.logical_and(h == my_head, q_split == my_split)

    def kv_copy(h):
        return remote(kv_send.at[h], kv_in.at[me], kv_s.at[h], kv_r.at[me], member(h, my_split))

    def kv_own(h):
        return pltpu.make_async_copy(kv_send.at[h], kv_in.at[me], kv_s.at[h])

    twin = my_split + 1 - 2 * lax.rem(my_split, 2)

    def step_split(k):
        return lax.rem(my_split + 2 * k, splits)

    def hand_copy(i, k):
        piece = i * splits + my_split
        return remote(kv_in.at[piece], kv_in.at[piece], hand_s.at[k, i], kv_r.at[piece],
                      member(my_head, step_split(k)))

    def twin_copy(i, k):
        piece = i * splits + step_split(k)
        return remote(kv_in.at[piece], kv_in.at[piece], side_s.at[k, i], kv_r.at[piece], member(my_head, twin))

    def kv_wait(piece):
        remote(kv_in.at[piece], kv_in.at[piece], kv_s.at[0], kv_r.at[piece], member(my_head, twin)).wait_recv()

    def dq_copy(kind, j, sub):
        piece = chunk_of(kind) * per + sub
        return remote(dq_send.at[kind, j, sub], dq_in.at[my_head, j], dq_s.at[kind, j, sub], dq_r.at[my_head, j],
                      source(piece))

    def dq_own(kind, j, sub):
        return pltpu.make_async_copy(dq_send.at[kind, j, sub], dq_in.at[my_head, j], dq_s.at[kind, j, sub])

    def has(split, b):
        return top - rank_of(split) >= b

    side = lax.rem(my_split, 2)

    def mate_copy(b, u):
        at = pl.ds(pl.multiple_of((2 * u + 1 - side) * tokens, tokens), tokens)
        return remote(acc_ref.at[b, at, :], mate_in.at[b, u], mate_s.at[b, u], mate_r.at[b, u],
                      member(my_head, twin))

    def mate_wait(b, u):
        landing = mate_in.at[b, u]
        remote(landing, landing, mate_s.at[b, u], mate_r.at[b, u], member(my_head, twin)).wait_recv()

    def red_copy(piece):
        return remote(part_ref.at[piece], red_in.at[my_split // 2, piece // splits], red_s.at[piece],
                      red_r.at[my_split // 2, piece // splits], member(my_head, lax.rem(piece, splits)))

    def fin_copy(i):
        return remote(fin_ref.at[i], dkv_in.at[my_head], fin_s.at[i], fin_r.at[my_head],
                      source(i * splits + my_split))

    def fin_own(i):
        return pltpu.make_async_copy(fin_ref.at[i], dkv_in.at[my_head], fin_s.at[i])

    barrier = pltpu.get_barrier_semaphore()
    everyone = lax.axis_size("span") * seq_count

    def greet(d, _):
        @pl.when(d != me)
        def _():
            pl.semaphore_signal(barrier, inc=1, device_id=source(d), device_id_type=MESH)
        return 0

    lax.fori_loop(0, everyone, greet, 0)

    for h in range(kv_heads):
        at = slice(h * HEAD_WIDTH, (h + 1) * HEAD_WIDTH)
        kv_send[h] = jnp.concatenate([k_ref[0, :, at], v_ref[0, :, at]], axis=1)
    for h in range(kv_heads):
        for j in range(heads):
            one = h * heads + j
            at = slice(one * HEAD_WIDTH, (one + 1) * HEAD_WIDTH)
            qg_send[h, j] = jnp.concatenate([q_ref[0, :, at], g_ref[0, :, at]], axis=1)
    product = o_ref[0].astype(jnp.float32) * g_ref[0].astype(jnp.float32)
    high = product.astype(jnp.bfloat16)
    low = (product - high.astype(jnp.float32)).astype(jnp.bfloat16)
    wide = kv_heads * heads * HEAD_WIDTH
    row = lax.broadcasted_iota(jnp.int32, (kv_heads * 8, wide), 0)
    column = lax.broadcasted_iota(jnp.int32, (kv_heads * 8, wide), 1) // HEAD_WIDTH
    ones = jnp.where(row == (column // heads) * 8 + lax.rem(column, heads), 1.0, 0.0).astype(jnp.bfloat16)
    dl_send[...] = (dot(ones, high, (1, 1)) + dot(ones, low, (1, 1))).reshape(kv_heads, 8, tokens)

    def clear(b, _):
        acc_ref[b] = jnp.zeros((chunk, PAIR), jnp.float32)
        return 0

    lax.fori_loop(0, 2 * splits, clear, 0)
    pl.semaphore_wait(barrier, everyone - 1)

    def qg_start(j):
        for t in range(kv_heads):
            h = far(my_head, t)
            other(q_mine(h), lambda: qg_copy(h, j).start(), lambda: qg_own(h, j).start())

    for t in range(kv_heads):
        h = far(my_head, t)
        other(h == my_head, lambda: kv_copy(h).start(), lambda: kv_own(h).start())
    qg_start(0)
    for t in range(kv_heads):
        h = far(my_head, t)
        other(q_mine(h), lambda: dl_copy(h).start(), lambda: dl_own(h).start())

    def hand_on(t, _):
        i = far(my_head, t)
        piece = i * splits + my_split
        other(piece == me, lambda: kv_wait(piece), lambda: kv_own(my_head).wait())
        twin_copy(i, 0).start()
        for k in range(1, splits // 2):
            hand_copy(i, k).start()
        return 0

    lax.fori_loop(0, kv_heads, hand_on, 0)

    def pass_on(i, _):
        for k in range(1, splits // 2):
            kv_wait(i * splits + step_split(k))
            twin_copy(i, k).start()
        return 0

    lax.fori_loop(0, kv_heads, pass_on, 0)

    def twin_wait(i, _):
        for k in range(splits // 2):
            kv_wait(i * splits + lax.rem(twin + 2 * k, splits))
        return 0

    lax.fori_loop(0, kv_heads, twin_wait, 0)

    lane = lax.broadcasted_iota(jnp.int32, (1, PAIR), 1)

    def kv_block(b):
        return kv_in[pl.ds(b * per, per)].reshape(chunk, PAIR)

    def hide(s):
        k_pos = lax.broadcasted_iota(jnp.int32, (chunk, chunk), 0)
        q_pos = lax.broadcasted_iota(jnp.int32, (chunk, chunk), 1)
        return jnp.where(k_pos <= q_pos, s, NEG_LARGE)

    def scores(kind, b, j, last):
        s = dot(kv_block(b), q_pad[kind, j], (1, 1))
        return hide(s) if last else s

    def slot(kind, b):
        return (my_rank + 1) * kind + b

    def stats(kind, j):
        c_q = chunk_of(kind)
        for sub in range(per):
            mine = c_q * per + sub == me
            landing = qg_in.at[kind, j, sub]
            other(mine,
                  lambda: remote(landing, landing, qg_s.at[0, j], qg_r.at[kind, j, sub],
                                 member(my_head, twin)).wait_recv(),
                  lambda: qg_own(my_head, j).wait())
        both = qg_in[kind, j].reshape(chunk, PAIR)
        q_pad[kind, j] = jnp.where(lane < HEAD_WIDTH, both, jnp.zeros_like(both))
        g_pad[kind, j] = jnp.where(lane < HEAD_WIDTH, jnp.zeros_like(both), both)
        dqt_ref[kind, j] = jnp.zeros((HEAD_WIDTH, chunk), jnp.float32)
        m_ref[kind, j] = jnp.full((1, chunk), NEG_LARGE, jnp.float32)
        l_ref[kind, j] = jnp.zeros((1, chunk), jnp.float32)

        def block(b, last):
            s = scores(kind, b, j, last)
            if resident:
                s_ref[slot(kind, b)] = s
            m_old = m_ref[kind, j]
            m_new = jnp.maximum(m_old, jnp.max(s, axis=0, keepdims=True))
            e = jnp.exp2((s - m_new) * factor)
            l_ref[kind, j] = (l_ref[kind, j] * jnp.exp2((m_old - m_new) * factor)
                              + jnp.sum(e, axis=0, keepdims=True))
            m_ref[kind, j] = m_new
            return 0

        lax.fori_loop(0, c_q, lambda b, _: block(b, False), 0)
        block(c_q, True)
        m_ref[kind, j] = m_ref[kind, j] * factor + jnp.log2(l_ref[kind, j])

    def grads(kind, j, b, last):
        kv = kv_block(b)
        s = s_ref[slot(kind, b)] if resident else scores(kind, b, j, last)
        p = jnp.exp2(s * factor - m_ref[kind, j])
        dp = dot(kv, g_pad[kind, j], (1, 1))
        ds = (p * (dp - dl_row[kind, j])).astype(jnp.bfloat16)
        acc_ref[b] += dot(ds, q_pad[kind, j], (1, 0)) + dot(p.astype(jnp.bfloat16), g_pad[kind, j], (1, 0))
        dqt_ref[kind, j] += dot(kv[:, :HEAD_WIDTH].T, ds, (1, 0))

    def send_dq(kind, j):
        for sub in range(per):
            part = dqt_ref[kind, j, :, sub * tokens:(sub + 1) * tokens] * scaling
            dq_send[kind, j, sub] = part.astype(jnp.bfloat16)
        for sub in range(per):
            other(chunk_of(kind) * per + sub == me, lambda: dq_copy(kind, j, sub).start(),
                  lambda: dq_own(kind, j, sub).start())

    def job(kind, j):
        c_q = chunk_of(kind)
        lax.fori_loop(0, c_q, lambda b, _: (grads(kind, j, b, False), 0)[1], 0)
        grads(kind, j, c_q, True)
        send_dq(kind, j)

    weight = jnp.where(lane < HEAD_WIDTH, scaling, 1.0)

    def own_piece(b, u):
        return b * per + 2 * u + side

    def own_rows(u):
        return pl.ds(pl.multiple_of((2 * u + side) * tokens, tokens), tokens)

    def pair_sends(b, u):
        return jnp.logical_and(lax.rem(own_piece(b, u), splits) != my_split,
                               jnp.logical_or(has(my_split, b), has(twin, b)))

    def hand_out(b):
        for u in range(per // 2):
            mate_copy(b, u).start()

    def pair_sum(b):
        @pl.when(has(twin, b))
        def _():
            for u in range(per // 2):
                mate_wait(b, u)
                acc_ref[b, own_rows(u), :] += mate_in[b, u]

        for u in range(per // 2):
            @pl.when(pair_sends(b, u))
            def _():
                piece = own_piece(b, u)
                part_ref[piece] = (acc_ref[b, own_rows(u), :] * weight).astype(jnp.bfloat16)
                red_copy(piece).start()

    def reduce(b):
        for u in range(per // 2):
            piece = own_piece(b, u)

            @pl.when(lax.rem(piece, splits) == my_split)
            def _():
                i = piece // splits
                total = acc_ref.at[b, own_rows(u), :]
                total[...] = total[...] * weight

                def add(f, _):
                    @pl.when(jnp.logical_and(f != my_split // 2,
                                             jnp.logical_or(has(2 * f, b), has(2 * f + 1, b))))
                    def _():
                        landing = red_in.at[f, i]
                        remote(landing, landing, red_s.at[0], red_r.at[f, i], member(my_head, twin)).wait_recv()
                        total[...] += red_in[f, i].astype(jnp.float32)
                    return 0

                lax.fori_loop(0, splits // 2, add, 0)
                fin_ref[i] = total[...].astype(jnp.bfloat16)
                other(piece == me, lambda: fin_copy(i).start(), lambda: fin_own(i).start())

    for kind in range(2):
        c_q = chunk_of(kind)
        for sub in range(per):
            small = dl_in.at[kind, sub]
            other(c_q * per + sub == me,
                  lambda: remote(small, small, dl_s.at[0], dl_r.at[kind, sub], member(my_head, twin)).wait_recv(),
                  lambda: dl_own(my_head).wait())
        for j in range(heads):
            for sub in range(per):
                dl_row[kind, j, :, sub * tokens:(sub + 1) * tokens] = dl_in[kind, sub, pl.ds(j, 1), :]

    def whole_head(j, _):
        stats(0, j)
        qg_start(j + 1)
        stats(1, j)
        for kind in range(2):
            job(kind, j)
        return 0

    lax.fori_loop(0, heads - 1, whole_head, 0)
    final = heads - 1
    for kind in range(2):
        stats(kind, final)
    job(0, final)

    def sweep(t, _):
        b = top - t

        @pl.when(b < chunk_of(1))
        def _():
            grads(1, final, b, False)

        @pl.when(b == chunk_of(1))
        def _():
            grads(1, final, b, True)

        @pl.when(b <= chunk_of(1))
        def _():
            hand_out(b)

        @pl.when(t > 0)
        def _():
            pair_sum(b + 1)

        @pl.when(t > 1)
        def _():
            reduce(b + 2)
        return 0

    lax.fori_loop(0, top + 1, sweep, 0)
    send_dq(1, final)
    pair_sum(0)
    reduce(1)
    reduce(0)

    for h in range(kv_heads):
        for j in range(heads):
            mine = q_mine(h)
            landing = dq_in.at[h, j]
            other(mine,
                  lambda: remote(landing, landing, dq_s.at[0, j, 0], dq_r.at[h, j], member(my_head, twin)).wait_recv(),
                  lambda: dq_own(my_kind, j, my_sub).wait())
    for h in range(kv_heads):
        landing = dkv_in.at[h]
        other(h == my_head,
              lambda: remote(landing, landing, fin_s.at[0], fin_r.at[h], member(my_head, twin)).wait_recv(),
              lambda: fin_own(my_head).wait())
    for h in range(kv_heads):
        @pl.when(h != my_head)
        def _():
            kv_copy(h).wait_send()

        @pl.when(jnp.logical_not(q_mine(h)))
        def _():
            dl_copy(h).wait_send()
            for j in range(heads):
                qg_copy(h, j).wait_send()

    def sent(i, _):
        for k in range(splits // 2):
            twin_copy(i, k).wait_send()
            if k:
                hand_copy(i, k).wait_send()

        @pl.when(i != my_head)
        def _():
            fin_copy(i).wait_send()
        return 0

    lax.fori_loop(0, kv_heads, sent, 0)
    for kind in range(2):
        for j in range(heads):
            for sub in range(per):
                @pl.when(chunk_of(kind) * per + sub != me)
                def _():
                    dq_copy(kind, j, sub).wait_send()

    def red_sent(b, _):
        for u in range(per // 2):
            @pl.when(has(my_split, b))
            def _():
                mate_copy(b, u).wait_send()

            @pl.when(pair_sends(b, u))
            def _():
                red_copy(own_piece(b, u)).wait_send()
        return 0

    lax.fori_loop(0, top + 1, red_sent, 0)


def results(dq_in, dkv_in, dq_out, dk_out, dv_out):
    kv_heads, heads, _, tokens = dq_in.shape
    dq_out[0] = dq_in[...].reshape(kv_heads * heads * HEAD_WIDTH, tokens).T
    for h in range(0, kv_heads, 2):
        at = slice(h * HEAD_WIDTH, (h + 2) * HEAD_WIDTH)
        dk_out[0, :, at] = jnp.concatenate([dkv_in[h, :, :HEAD_WIDTH], dkv_in[h + 1, :, :HEAD_WIDTH]], axis=1)
        dv_out[0, :, at] = jnp.concatenate([dkv_in[h, :, HEAD_WIDTH:], dkv_in[h + 1, :, HEAD_WIDTH:]], axis=1)


def vmem(count):
    return [pl.BlockSpec(memory_space=pltpu.VMEM)] * count


def per_device(queries, key_head_matrix, value_head_matrix, attn_output, out_grad):
    seq_count = lax.axis_size("seq")
    tokens = queries.shape[1]
    kv_heads = key_head_matrix.shape[2] // HEAD_WIDTH
    splits = lax.axis_size("span") // kv_heads * seq_count
    pieces = kv_heads * splits
    heads = QUERY_PER_KEY
    per = kv_heads // 2
    chunk = per * tokens
    count = 2 * splits + 1
    resident = count * chunk * chunk * 4 <= SCORE_BYTES
    dma = pltpu.SemaphoreType.DMA
    low, full = jnp.bfloat16, jnp.float32
    dq, dkv = pl.pallas_call(
        functools.partial(kernel, kv_heads, resident),
        out_shape=(
            jax.ShapeDtypeStruct((kv_heads, heads, HEAD_WIDTH, tokens), low),
            jax.ShapeDtypeStruct((kv_heads, tokens, PAIR), low),
        ),
        in_specs=vmem(5),
        out_specs=tuple(vmem(2)),
        scratch_shapes=[
            pltpu.VMEM((kv_heads, heads, tokens, PAIR), low),
            pltpu.VMEM((kv_heads, tokens, PAIR), low),
            pltpu.VMEM((kv_heads, 8, tokens), full),
            pltpu.VMEM((2, heads, per, tokens, PAIR), low),
            pltpu.VMEM((pieces, tokens, PAIR), low),
            pltpu.VMEM((2, per, 8, tokens), full),
            pltpu.VMEM((2, heads, chunk, PAIR), low),
            pltpu.VMEM((2, heads, chunk, PAIR), low),
            pltpu.VMEM((2, heads, 1, chunk), full),
            pltpu.VMEM((count, chunk, chunk) if resident else (1, 8, chunk), full),
            pltpu.VMEM((2, heads, 1, chunk), full),
            pltpu.VMEM((2, heads, 1, chunk), full),
            pltpu.VMEM((2, heads, HEAD_WIDTH, chunk), full),
            pltpu.VMEM((2 * splits, chunk, PAIR), full),
            pltpu.VMEM((2, heads, per, HEAD_WIDTH, tokens), low),
            pltpu.VMEM((2 * splits, per // 2, tokens, PAIR), full),
            pltpu.VMEM((pieces, tokens, PAIR), low),
            pltpu.VMEM((splits // 2, kv_heads, tokens, PAIR), low),
            pltpu.VMEM((kv_heads, tokens, PAIR), low),
            dma((kv_heads, heads)),
            dma((2, heads, per)),
            dma((kv_heads,)),
            dma((pieces,)),
            dma((kv_heads,)),
            dma((2, per)),
            dma((splits // 2, kv_heads)),
            dma((splits // 2, kv_heads)),
            dma((2, heads, per)),
            dma((kv_heads, heads)),
            dma((2 * splits, per // 2)),
            dma((2 * splits, per // 2)),
            dma((pieces,)),
            dma((splits // 2, kv_heads)),
            dma((kv_heads,)),
            dma((kv_heads,)),
        ],
        compiler_params=pltpu.CompilerParams(collective_id=0, has_side_effects=True, vmem_limit_bytes=60 * 2**20),
        name="attention_grads",
    )(queries, key_head_matrix, value_head_matrix, attn_output, out_grad)
    return pl.pallas_call(
        results,
        out_shape=(
            jax.ShapeDtypeStruct(queries.shape, low),
            jax.ShapeDtypeStruct(key_head_matrix.shape, low),
            jax.ShapeDtypeStruct(value_head_matrix.shape, low),
        ),
        in_specs=vmem(2),
        out_specs=tuple(vmem(3)),
        name="results",
    )(dq, dkv)


def solution(mesh):
    spec = P("span", "seq", None)
    return jax.shard_map(
        per_device, mesh=mesh, in_specs=(spec,) * 5, out_specs=(spec,) * 3, check_vma=False
    )
```

time: 89.6 us -> 77.8 us (0.87)
  Pallas kernels: 84.7 us -> 77 us
  local copies, waits for them, and re-layouts: 3.41 us -> 0 us
    pallas_call x1, Pallas kernels: 84.7 us -> 74.9 us  [per_device(): pl.pallas_call(functools.partial(kernel, kv_heads, resident), out_shape=(...]
    unnamed x7 -> x0, local copies, waits for them, and re-layouts: 3.41 us -> none
    pallas_call x0 -> x1, Pallas kernels: none -> 2.05 us  [per_device(): pl.pallas_call(results, out_shape=(jax.ShapeDtypeStruct(queries.shape, lo...]
where the time goes in v2:
time: 77.8 us; the launch traced here: 77.6 us
  Pallas kernels  77 us (99%)
    pallas_call x1, Pallas kernels, per_device(): pl.pallas_call(functools.partial(kernel, kv_heads, resident), out_shape=(...  74.9 us
    pallas_call x1, Pallas kernels, per_device(): pl.pallas_call(results, out_shape=(jax.ShapeDtypeStruct(queries.shape, lo...  2.05 us

profile of v2, /device:TPU:0, one launch (start us, length us, event | category | flops | bytes accessed | tf_op | source)
XLA Modules:
  0.0 77.6 jit_solution(13052974681671805119)
XLA Ops:
  0.6 74.9 %attention_grads.1 = (bf16[8,3,64,128]{3,2,1,0:T(8,128)(2,1)}, bf16[8,128,128]{2,1,0:T(8,128)(2,1)}) custom-call(bf16[1,128,1536]{2,1,0:T(8,128)(2,1)} %q_ref.1, bf16[1,128,512]{2,1,0:T(8,128)(2,1)} %k_ref.1, bf16[1,128,512]{2,1,0:T(8,128)(2,1)} %v_ref.1, bf16[1,128,1536]{2,1,0:T(8,128)(2,1)} %o_ref.1, bf16[1,128,1536]{2,1,0:T(8,128)(2,1)} %g_ref.1), custom_call_target="tpu_custom_call" | custom-call | tf_op jit(solution)/shard_map/attention_grads/pallas_call | solution.py:494
  75.6 2.1 %results.1 = (bf16[1,128,1536]{2,1,0:T(8,128)(2,1)}, bf16[1,128,512]{2,1,0:T(8,128)(2,1)}, bf16[1,128,512]{2,1,0:T(8,128)(2,1)}) custom-call(bf16[8,3,64,128]{3,2,1,0:T(8,128)(2,1)} %get-tuple-element.5.dq_in, bf16[8,128,128]{2,1,0:T(8,128)(2,1)} %get-tuple-element.6.dkv_in), custom_call_target="tpu_custom_call" | custom-call | tf_op jit(solution)/shard_map/results/pallas_call | solution.py:542

commit v3 on v2

--- a/solution.py
+++ b/solution.py
@@ -15,6 +15,8 @@
 MESH = pl.DeviceIdType.MESH
 LOG2E = math.log2(math.e)
 SCORE_BYTES = 30 * 2**20
+SUM_LAG = 2
+REDUCE_LAG = 5
 
 
 def dot(a, b, contract):
@@ -22,7 +24,7 @@
 
 
 def kernel(kv_heads, resident, q_ref, k_ref, v_ref, o_ref, g_ref, dq_in, dkv_in,
-           qg_send, kv_send, dl_send, qg_in, kv_in, dl_in, q_pad, g_pad, dl_row, s_ref, m_ref, l_ref, dqt_ref,
+           qg_send, kv_send, dl_send, qg_in, kv_in, dl_in, q_pad, g_pad, dl_row, s0_ref, s1_ref, p0_ref, p1_ref, ds0_ref, ds1_ref, m_ref, dqt_ref,
            acc_ref, dq_send, mate_in, part_ref, red_in, fin_ref,
            qg_s, qg_r, kv_s, kv_r, dl_s, dl_r, side_s, hand_s, dq_s, dq_r, mate_s, mate_r, red_s, red_r, fin_s, fin_r):
     seq_count = lax.axis_size("seq")
@@ -231,20 +233,27 @@
 
     lane = lax.broadcasted_iota(jnp.int32, (1, PAIR), 1)
 
-    def kv_block(b):
-        return kv_in[pl.ds(b * per, per)].reshape(chunk, PAIR)
-
-    def hide(s):
-        k_pos = lax.broadcasted_iota(jnp.int32, (chunk, chunk), 0)
-        q_pos = lax.broadcasted_iota(jnp.int32, (chunk, chunk), 1)
+    half = chunk // 2
+    s_refs = (s0_ref, s1_ref)
+    p_refs = (p0_ref, p1_ref)
+    ds_refs = (ds0_ref, ds1_ref)
+
+    def kv_half(b, side_of):
+        return kv_in[pl.ds(b * per + side_of * (per // 2), per // 2)].reshape(half, PAIR)
+
+    def hide(s, side_of):
+        k_pos = side_of * half + lax.broadcasted_iota(jnp.int32, (half, chunk), 0)
+        q_pos = lax.broadcasted_iota(jnp.int32, (half, chunk), 1)
         return jnp.where(k_pos <= q_pos, s, NEG_LARGE)
 
-    def scores(kind, b, j, last):
-        s = dot(kv_block(b), q_pad[kind, j], (1, 1))
-        return hide(s) if last else s
+    def scores(kind, j, b, side_of):
+        return dot(kv_half(b, side_of), q_pad[kind, j], (1, 1))
+
+    def top_of(s):
+        return jnp.max(s, axis=0, keepdims=True)
 
     def slot(kind, b):
-        return (my_rank + 1) * kind + b
+        return (my_rank + 1) * kind + b if resident else 0
 
     def stats(kind, j):
         c_q = chunk_of(kind)
@@ -259,33 +268,65 @@
         q_pad[kind, j] = jnp.where(lane < HEAD_WIDTH, both, jnp.zeros_like(both))
         g_pad[kind, j] = jnp.where(lane < HEAD_WIDTH, jnp.zeros_like(both), both)
         dqt_ref[kind, j] = jnp.zeros((HEAD_WIDTH, chunk), jnp.float32)
-        m_ref[kind, j] = jnp.full((1, chunk), NEG_LARGE, jnp.float32)
-        l_ref[kind, j] = jnp.zeros((1, chunk), jnp.float32)
-
-        def block(b, last):
-            s = scores(kind, b, j, last)
-            if resident:
-                s_ref[slot(kind, b)] = s
-            m_old = m_ref[kind, j]
-            m_new = jnp.maximum(m_old, jnp.max(s, axis=0, keepdims=True))
-            e = jnp.exp2((s - m_new) * factor)
-            l_ref[kind, j] = (l_ref[kind, j] * jnp.exp2((m_old - m_new) * factor)
-                              + jnp.sum(e, axis=0, keepdims=True))
-            m_ref[kind, j] = m_new
-            return 0
-
-        lax.fori_loop(0, c_q, lambda b, _: block(b, False), 0)
-        block(c_q, True)
-        m_ref[kind, j] = m_ref[kind, j] * factor + jnp.log2(l_ref[kind, j])
-
-    def grads(kind, j, b, last):
-        kv = kv_block(b)
-        s = s_ref[slot(kind, b)] if resident else scores(kind, b, j, last)
+
+        def make(b, side_of):
+            s = scores(kind, j, b, side_of)
+            s_refs[side_of][slot(kind, b)] = s
+            return top_of(s)
+
+        def take(b, side_of, seen, m_old, l_old):
+            m_new = jnp.maximum(m_old, seen)
+            e = jnp.exp2((s_refs[side_of][slot(kind, b)] - m_new) * factor)
+            l_new = l_old * jnp.exp2((m_old - m_new) * factor) + jnp.sum(e, axis=0, keepdims=True)
+            return m_new, l_new
+
+        def block(b, carry):
+            seen, m, l = carry
+            later = make(b, 1)
+            m, l = take(b, 0, seen, m, l)
+            following = make(b + 1, 0)
+            m, l = take(b, 1, later, m, l)
+            return following, m, l
+
+        start = (make(0, 0), jnp.full((1, chunk), NEG_LARGE, jnp.float32), jnp.zeros((1, chunk), jnp.float32))
+        _, m, l = lax.fori_loop(0, c_q, block, start)
+        make(c_q, 1)
+        for side_of in range(2):
+            s = hide(s_refs[side_of][slot(kind, c_q)], side_of)
+            s_refs[side_of][slot(kind, c_q)] = s
+            m, l = take(c_q, side_of, top_of(s), m, l)
+        m_ref[kind, j] = m * factor + jnp.log2(l)
+
+    def weigh(kind, j, b, side_of):
+        kv = kv_half(b, side_of)
+        if resident:
+            s = s_refs[side_of][slot(kind, b)]
+        else:
+            s = scores(kind, j, b, side_of)
+            k_pos = b * chunk + side_of * half + lax.broadcasted_iota(jnp.int32, (half, chunk), 0)
+            q_pos = chunk_of(kind) * chunk + lax.broadcasted_iota(jnp.int32, (half, chunk), 1)
+            s = jnp.where(k_pos <= q_pos, s, NEG_LARGE)
         p = jnp.exp2(s * factor - m_ref[kind, j])
         dp = dot(kv, g_pad[kind, j], (1, 1))
-        ds = (p * (dp - dl_row[kind, j])).astype(jnp.bfloat16)
-        acc_ref[b] += dot(ds, q_pad[kind, j], (1, 0)) + dot(p.astype(jnp.bfloat16), g_pad[kind, j], (1, 0))
-        dqt_ref[kind, j] += dot(kv[:, :HEAD_WIDTH].T, ds, (1, 0))
+        ds_refs[side_of][...] = (p * (dp - dl_row[kind, j])).astype(jnp.bfloat16)
+        p_refs[side_of][...] = p.astype(jnp.bfloat16)
+
+    def gather(kind, j, b, side_of):
+        ds = ds_refs[side_of][...]
+        at = pl.ds(side_of * half, half)
+        acc_ref[b, at, :] += dot(ds, q_pad[kind, j], (1, 0)) + dot(p_refs[side_of][...], g_pad[kind, j], (1, 0))
+        dqt_ref[kind, j] += dot(kv_half(b, side_of)[:, :HEAD_WIDTH].T, ds, (1, 0))
+
+    def open_job(kind, j, b):
+        weigh(kind, j, b, 0)
+        weigh(kind, j, b, 1)
+        gather(kind, j, b, 0)
+
+    def next_block(kind, j, before, b):
+        weigh(kind, j, b, 0)
+        gather(kind, j, before, 1)
+        weigh(kind, j, b, 1)
+        gather(kind, j, b, 0)
 
     def send_dq(kind, j):
         for sub in range(per):
@@ -297,8 +338,9 @@
 
     def job(kind, j):
         c_q = chunk_of(kind)
-        lax.fori_loop(0, c_q, lambda b, _: (grads(kind, j, b, False), 0)[1], 0)
-        grads(kind, j, c_q, True)
+        open_job(kind, j, 0)
+        lax.fori_loop(1, c_q + 1, lambda b, _: (next_block(kind, j, b - 1, b), 0)[1], 0)
+        gather(kind, j, c_q, 1)
         send_dq(kind, j)
 
     weight = jnp.where(lane < HEAD_WIDTH, scaling, 1.0)
@@ -379,35 +421,86 @@
         stats(kind, final)
     job(0, final)
 
+    def turn(t):
+        return jnp.where(t < splits, top - t, lax.rem(t + my_head, splits))
+
+    def tidy(t, _):
+        @pl.when(t >= SUM_LAG)
+        def _():
+            pair_sum(turn(t - SUM_LAG))
+
+        @pl.when(t >= REDUCE_LAG)
+        def _():
+            reduce(turn(t - REDUCE_LAG))
+        return 0
+
     def sweep(t, _):
-        b = top - t
-
-        @pl.when(b < chunk_of(1))
-        def _():
-            grads(1, final, b, False)
-
-        @pl.when(b == chunk_of(1))
-        def _():
-            grads(1, final, b, True)
-
-        @pl.when(b <= chunk_of(1))
-        def _():
-            hand_out(b)
-
-        @pl.when(t > 0)
-        def _():
-            pair_sum(b + 1)
-
-        @pl.when(t > 1)
-        def _():
-            reduce(b + 2)
-        return 0
-
-    lax.fori_loop(0, top + 1, sweep, 0)
+        next_block(1, final, turn(t - 1), turn(t))
+        hand_out(turn(t - 1))
+        return tidy(t, 0)
+
+    def late_sum(t, _):
+        pair_sum(turn(t))
+        return 0
+
+    def late_reduce(t, _):
+        reduce(turn(t))
+        return 0
+
+    lax.fori_loop(0, my_rank + 1, tidy, 0)
+    open_job(1, final, chunk_of(1))
+    lax.fori_loop(my_rank + 1, top + 1, sweep, 0)
+    gather(1, final, turn(top), 1)
+    hand_out(turn(top))
     send_dq(1, final)
-    pair_sum(0)
-    reduce(1)
-    reduce(0)
+    middle = top + 1 - SUM_LAG
+    start = max(0, top + 1 - REDUCE_LAG)
+    lax.fori_loop(start, middle, late_reduce, 0)
+    lax.fori_loop(middle, top + 1, late_sum, 0)
+    lax.fori_loop(middle, top + 1, late_reduce, 0)
+
+    for h in range(kv_heads):
+        @pl.when(h != my_head)
+        def _():
+            kv_copy(h).wait_send()
+
+        @pl.when(jnp.logical_not(q_mine(h)))
+        def _():
+            dl_copy(h).wait_send()
+            for j in range(heads):
+                qg_copy(h, j).wait_send()
+
+    def sent(i, _):
+        for k in range(splits // 2):
+            twin_copy(i, k).wait_send()
+            if k:
+                hand_copy(i, k).wait_send()
+
+        @pl.when(i != my_head)
+        def _():
+            fin_copy(i).wait_send()
+        return 0
+
+    lax.fori_loop(0, kv_heads, sent, 0)
+    for kind in range(2):
+        for j in range(heads):
+            for sub in range(per):
+                @pl.when(chunk_of(kind) * per + sub != me)
+                def _():
+                    dq_copy(kind, j, sub).wait_send()
+
+    def red_sent(b, _):
+        for u in range(per // 2):
+            @pl.when(has(my_split, b))
+            def _():
+                mate_copy(b, u).wait_send()
+
+            @pl.when(pair_sends(b, u))
+            def _():
+                red_copy(own_piece(b, u)).wait_send()
+        return 0
+
+    lax.fori_loop(0, top + 1, red_sent, 0)
 
     for h in range(kv_heads):
         for j in range(heads):
@@ -421,48 +514,6 @@
         other(h == my_head,
               lambda: remote(landing, landing, fin_s.at[0], fin_r.at[h], member(my_head, twin)).wait_recv(),
               lambda: fin_own(my_head).wait())
-    for h in range(kv_heads):
-        @pl.when(h != my_head)
-        def _():
-            kv_copy(h).wait_send()
-
-        @pl.when(jnp.logical_not(q_mine(h)))
-        def _():
-            dl_copy(h).wait_send()
-            for j in range(heads):
-                qg_copy(h, j).wait_send()
-
-    def sent(i, _):
-        for k in range(splits // 2):
-            twin_copy(i, k).wait_send()
-            if k:
-                hand_copy(i, k).wait_send()
-
-        @pl.when(i != my_head)
-        def _():
-            fin_copy(i).wait_send()
-        return 0
-
-    lax.fori_loop(0, kv_heads, sent, 0)
-    for kind in range(2):
-        for j in range(heads):
-            for sub in range(per):
-                @pl.when(chunk_of(kind) * per + sub != me)
-                def _():
-                    dq_copy(kind, j, sub).wait_send()
-
-    def red_sent(b, _):
-        for u in range(per // 2):
-            @pl.when(has(my_split, b))
-            def _():
-                mate_copy(b, u).wait_send()
-
-            @pl.when(pair_sends(b, u))
-            def _():
-                red_copy(own_piece(b, u)).wait_send()
-        return 0
-
-    lax.fori_loop(0, top + 1, red_sent, 0)
 
 
 def results(dq_in, dkv_in, dq_out, dk_out, dv_out):
@@ -489,6 +540,7 @@
     chunk = per * tokens
     count = 2 * splits + 1
     resident = count * chunk * chunk * 4 <= SCORE_BYTES
+    count = count if resident else 1
     dma = pltpu.SemaphoreType.DMA
     low, full = jnp.bfloat16, jnp.float32
     dq, dkv = pl.pallas_call(
@@ -509,8 +561,12 @@
             pltpu.VMEM((2, heads, chunk, PAIR), low),
             pltpu.VMEM((2, heads, chunk, PAIR), low),
             pltpu.VMEM((2, heads, 1, chunk), full),
-            pltpu.VMEM((count, chunk, chunk) if resident else (1, 8, chunk), full),
-            pltpu.VMEM((2, heads, 1, chunk), full),
+            pltpu.VMEM((count, chunk // 2, chunk), full),
+            pltpu.VMEM((count, chunk // 2, chunk), full),
+            pltpu.VMEM((chunk // 2, chunk), low),
+            pltpu.VMEM((chunk // 2, chunk), low),
+            pltpu.VMEM((chunk // 2, chunk), low),
+            pltpu.VMEM((chunk // 2, chunk), low),
             pltpu.VMEM((2, heads, 1, chunk), full),
             pltpu.VMEM((2, heads, HEAD_WIDTH, chunk), full),
             pltpu.VMEM((2 * splits, chunk, PAIR), full),

time: 77.8 us -> 72.3 us (0.929)
  Pallas kernels: 77 us -> 71.5 us
    pallas_call x1, Pallas kernels: 74.9 us -> 69.5 us  [per_device(): pl.pallas_call(functools.partial(kernel, kv_heads, resident), out_shape=(...]
where the time goes in v3:
time: 72.3 us; the launch traced here: 72.2 us
  Pallas kernels  71.5 us (99%)
    pallas_call x1, Pallas kernels, per_device(): pl.pallas_call(functools.partial(kernel, kv_heads, resident), out_shape=(...  69.5 us
    pallas_call x1, Pallas kernels, per_device(): pl.pallas_call(results, out_shape=(jax.ShapeDtypeStruct(queries.shape, lo...  2.05 us

profile of v3, /device:TPU:0, one launch (start us, length us, event | category | flops | bytes accessed | tf_op | source)
XLA Modules:
  0.0 72.2 jit_solution(3286779256794280231)
XLA Ops:
  0.6 69.5 %attention_grads.1 = (bf16[8,3,64,128]{3,2,1,0:T(8,128)(2,1)}, bf16[8,128,128]{2,1,0:T(8,128)(2,1)}) custom-call(bf16[1,128,1536]{2,1,0:T(8,128)(2,1)} %q_ref.1, bf16[1,128,512]{2,1,0:T(8,128)(2,1)} %k_ref.1, bf16[1,128,512]{2,1,0:T(8,128)(2,1)} %v_ref.1, bf16[1,128,1536]{2,1,0:T(8,128)(2,1)} %o_ref.1, bf16[1,128,1536]{2,1,0:T(8,128)(2,1)} %g_ref.1), custom_call_target="tpu_custom_call" | custom-call | tf_op jit(solution)/shard_map/attention_grads/pallas_call | solution.py:546
  70.1 2.1 %results.1 = (bf16[1,128,1536]{2,1,0:T(8,128)(2,1)}, bf16[1,128,512]{2,1,0:T(8,128)(2,1)}, bf16[1,128,512]{2,1,0:T(8,128)(2,1)}) custom-call(bf16[8,3,64,128]{3,2,1,0:T(8,128)(2,1)} %get-tuple-element.5.dq_in, bf16[8,128,128]{2,1,0:T(8,128)(2,1)} %get-tuple-element.6.dkv_in), custom_call_target="tpu_custom_call" | custom-call | tf_op jit(solution)/shard_map/results/pallas_call | solution.py:598

commit v4 on v3

--- a/solution.py
+++ b/solution.py
@@ -23,17 +23,17 @@
     return lax.dot_general(a, b, ((contract[:1], contract[1:]), ((), ())), preferred_element_type=jnp.float32)
 
 
-def kernel(kv_heads, resident, q_ref, k_ref, v_ref, o_ref, g_ref, dq_in, dkv_in,
-           qg_send, kv_send, dl_send, qg_in, kv_in, dl_in, q_pad, g_pad, dl_row, s0_ref, s1_ref, p0_ref, p1_ref, ds0_ref, ds1_ref, m_ref, dqt_ref,
+def kernel(kv_heads, resident, q_far, k_far, v_far, o_far, g_far, dq_in, dkv_in,
+           q_ref, k_ref, v_ref, o_ref, g_ref, qg_send, kv_send, dl_send, qg_in, kv_in, dl_in, q_pad, g_pad, dl_row, s0_ref, s1_ref, p0_ref, p1_ref, ds0_ref, ds1_ref, m_ref, dqt_ref,
            acc_ref, dq_send, mate_in, part_ref, red_in, fin_ref,
-           qg_s, qg_r, kv_s, kv_r, dl_s, dl_r, side_s, hand_s, dq_s, dq_r, mate_s, mate_r, red_s, red_r, fin_s, fin_r):
+           in_s, qg_s, qg_r, kv_s, kv_r, dl_s, dl_r, side_s, hand_s, dq_s, dq_r, mate_s, mate_r, red_s, red_r, fin_s, fin_r):
     seq_count = lax.axis_size("seq")
     seq = lax.axis_index("seq")
     span = lax.axis_index("span")
     heads = QUERY_PER_KEY
     spread = lax.axis_size("span") // kv_heads
     splits = spread * seq_count
-    tokens = q_ref.shape[1]
+    tokens = q_far.shape[1]
     per = kv_heads // 2
     chunk = per * tokens
     top = 2 * splits - 1
@@ -167,6 +167,19 @@
         return 0
 
     lax.fori_loop(0, everyone, greet, 0)
+
+    loads = [pltpu.make_async_copy(far_one, near_one, in_s.at[n]) for n, (far_one, near_one) in enumerate(
+        ((k_far, k_ref), (v_far, v_ref), (q_far, q_ref), (g_far, g_ref), (o_far, o_ref)))]
+    for load in loads:
+        load.start()
+
+    def clear(b, _):
+        acc_ref[b] = jnp.zeros((chunk, PAIR), jnp.float32)
+        return 0
+
+    lax.fori_loop(0, 2 * splits, clear, 0)
+    for load in loads:
+        load.wait()
 
     for h in range(kv_heads):
         at = slice(h * HEAD_WIDTH, (h + 1) * HEAD_WIDTH)
@@ -185,11 +198,6 @@
     ones = jnp.where(row == (column // heads) * 8 + lax.rem(column, heads), 1.0, 0.0).astype(jnp.bfloat16)
     dl_send[...] = (dot(ones, high, (1, 1)) + dot(ones, low, (1, 1))).reshape(kv_heads, 8, tokens)
 
-    def clear(b, _):
-        acc_ref[b] = jnp.zeros((chunk, PAIR), jnp.float32)
-        return 0
-
-    lax.fori_loop(0, 2 * splits, clear, 0)
     pl.semaphore_wait(barrier, everyone - 1)
 
     def qg_start(j):
@@ -241,9 +249,9 @@
     def kv_half(b, side_of):
         return kv_in[pl.ds(b * per + side_of * (per // 2), per // 2)].reshape(half, PAIR)
 
-    def hide(s, side_of):
-        k_pos = side_of * half + lax.broadcasted_iota(jnp.int32, (half, chunk), 0)
-        q_pos = lax.broadcasted_iota(jnp.int32, (half, chunk), 1)
+    def hide(s):
+        k_pos = lax.broadcasted_iota(jnp.int32, s.shape, 0)
+        q_pos = lax.broadcasted_iota(jnp.int32, s.shape, 1)
         return jnp.where(k_pos <= q_pos, s, NEG_LARGE)
 
     def scores(kind, j, b, side_of):
@@ -290,26 +298,33 @@
 
         start = (make(0, 0), jnp.full((1, chunk), NEG_LARGE, jnp.float32), jnp.zeros((1, chunk), jnp.float32))
         _, m, l = lax.fori_loop(0, c_q, block, start)
-        make(c_q, 1)
-        for side_of in range(2):
-            s = hide(s_refs[side_of][slot(kind, c_q)], side_of)
-            s_refs[side_of][slot(kind, c_q)] = s
-            m, l = take(c_q, side_of, top_of(s), m, l)
+        s = hide(s_refs[0][slot(kind, c_q)])
+        s_refs[0][slot(kind, c_q)] = s
+        m, l = take(c_q, 0, top_of(s), m, l)
+        s = hide(dot(kv_half(c_q, 1), q_pad[kind, j, half:], (1, 1)))
+        s_refs[1][slot(kind, c_q), :, half:] = s
+        m_new = jnp.maximum(m, jnp.concatenate([m[:, :half], top_of(s)], axis=1))
+        e = jnp.sum(jnp.exp2((s - m_new[:, half:]) * factor), axis=0, keepdims=True)
+        l = l * jnp.exp2((m - m_new) * factor) + jnp.concatenate([jnp.zeros_like(e), e], axis=1)
+        m = m_new
         m_ref[kind, j] = m * factor + jnp.log2(l)
 
-    def weigh(kind, j, b, side_of):
+    def weigh(kind, j, b, side_of, first=0):
         kv = kv_half(b, side_of)
         if resident:
-            s = s_refs[side_of][slot(kind, b)]
+            s = s_refs[side_of][slot(kind, b), :, first:]
         else:
-            s = scores(kind, j, b, side_of)
-            k_pos = b * chunk + side_of * half + lax.broadcasted_iota(jnp.int32, (half, chunk), 0)
-            q_pos = chunk_of(kind) * chunk + lax.broadcasted_iota(jnp.int32, (half, chunk), 1)
+            s = dot(kv, q_pad[kind, j, first:], (1, 1))
+            k_pos = b * chunk + side_of * half + lax.broadcasted_iota(jnp.int32, s.shape, 0)
+            q_pos = chunk_of(kind) * chunk + first + lax.broadcasted_iota(jnp.int32, s.shape, 1)
             s = jnp.where(k_pos <= q_pos, s, NEG_LARGE)
-        p = jnp.exp2(s * factor - m_ref[kind, j])
-        dp = dot(kv, g_pad[kind, j], (1, 1))
-        ds_refs[side_of][...] = (p * (dp - dl_row[kind, j])).astype(jnp.bfloat16)
-        p_refs[side_of][...] = p.astype(jnp.bfloat16)
+        p = jnp.exp2(s * factor - m_ref[kind, j, :, first:])
+        dp = dot(kv, g_pad[kind, j, first:], (1, 1))
+        ds_refs[side_of][:, first:] = (p * (dp - dl_row[kind, j, :, first:])).astype(jnp.bfloat16)
+        p_refs[side_of][:, first:] = p.astype(jnp.bfloat16)
+        if first:
+            ds_refs[side_of][:, :first] = jnp.zeros((half, first), jnp.bfloat16)
+            p_refs[side_of][:, :first] = jnp.zeros((half, first), jnp.bfloat16)
 
     def gather(kind, j, b, side_of):
         ds = ds_refs[side_of][...]
@@ -317,9 +332,10 @@
         acc_ref[b, at, :] += dot(ds, q_pad[kind, j], (1, 0)) + dot(p_refs[side_of][...], g_pad[kind, j], (1, 0))
         dqt_ref[kind, j] += dot(kv_half(b, side_of)[:, :HEAD_WIDTH].T, ds, (1, 0))
 
-    def open_job(kind, j, b):
+    def open_job(kind, j):
+        b = chunk_of(kind)
         weigh(kind, j, b, 0)
-        weigh(kind, j, b, 1)
+        weigh(kind, j, b, 1, half)
         gather(kind, j, b, 0)
 
     def next_block(kind, j, before, b):
@@ -338,9 +354,9 @@
 
     def job(kind, j):
         c_q = chunk_of(kind)
-        open_job(kind, j, 0)
-        lax.fori_loop(1, c_q + 1, lambda b, _: (next_block(kind, j, b - 1, b), 0)[1], 0)
-        gather(kind, j, c_q, 1)
+        open_job(kind, j)
+        lax.fori_loop(1, c_q + 1, lambda t, _: (next_block(kind, j, c_q - t + 1, c_q - t), 0)[1], 0)
+        gather(kind, j, 0, 1)
         send_dq(kind, j)
 
     weight = jnp.where(lane < HEAD_WIDTH, scaling, 1.0)
@@ -448,7 +464,7 @@
         return 0
 
     lax.fori_loop(0, my_rank + 1, tidy, 0)
-    open_job(1, final, chunk_of(1))
+    open_job(1, final)
     lax.fori_loop(my_rank + 1, top + 1, sweep, 0)
     gather(1, final, turn(top), 1)
     hand_out(turn(top))
@@ -549,9 +565,14 @@
             jax.ShapeDtypeStruct((kv_heads, heads, HEAD_WIDTH, tokens), low),
             jax.ShapeDtypeStruct((kv_heads, tokens, PAIR), low),
         ),
-        in_specs=vmem(5),
+        in_specs=[pl.BlockSpec(memory_space=pl.ANY)] * 5,
         out_specs=tuple(vmem(2)),
         scratch_shapes=[
+            pltpu.VMEM(queries.shape, low),
+            pltpu.VMEM(key_head_matrix.shape, low),
+            pltpu.VMEM(key_head_matrix.shape, low),
+            pltpu.VMEM(queries.shape, low),
+            pltpu.VMEM(queries.shape, low),
             pltpu.VMEM((kv_heads, heads, tokens, PAIR), low),
             pltpu.VMEM((kv_heads, tokens, PAIR), low),
             pltpu.VMEM((kv_heads, 8, tokens), full),
@@ -575,8 +596,9 @@
             pltpu.VMEM((pieces, tokens, PAIR), low),
             pltpu.VMEM((splits // 2, kv_heads, tokens, PAIR), low),
             pltpu.VMEM((kv_heads, tokens, PAIR), low),
-            dma((kv_heads, heads)),
-            dma((2, heads, per)),
+            dma((5,)),
+            dma((kv_heads, heads + 1)),
+            dma((2, heads + 1, per)),
             dma((kv_heads,)),
             dma((pieces,)),
             dma((kv_heads,)),

time: 72.3 us -> 71 us (0.982)
  Pallas kernels: 71.5 us -> 70.2 us
    pallas_call x1, Pallas kernels: 69.5 us -> 68.1 us  [per_device(): pl.pallas_call(functools.partial(kernel, kv_heads, resident), out_shape=(...]
where the time goes in v4:
time: 71 us; the launch traced here: 70.8 us
  Pallas kernels  70.2 us (99%)
    pallas_call x1, Pallas kernels, per_device(): pl.pallas_call(functools.partial(kernel, kv_heads, resident), out_shape=(...  68.1 us
    pallas_call x1, Pallas kernels, per_device(): pl.pallas_call(results, out_shape=(jax.ShapeDtypeStruct(queries.shape, lo...  2.05 us

profile of v4, /device:TPU:0, one launch (start us, length us, event | category | flops | bytes accessed | tf_op | source)
XLA Modules:
  0.0 70.8 jit_solution(15586947548321441121)
XLA Ops:
  0.6 68.1 %attention_grads.1 = (bf16[8,3,64,128]{3,2,1,0:T(8,128)(2,1)}, bf16[8,128,128]{2,1,0:T(8,128)(2,1)}) custom-call(bf16[1,128,1536]{2,1,0:T(8,128)(2,1)} %q_far.1, bf16[1,128,512]{2,1,0:T(8,128)(2,1)} %k_far.1, bf16[1,128,512]{2,1,0:T(8,128)(2,1)} %v_far.1, bf16[1,128,1536]{2,1,0:T(8,128)(2,1)} %o_far.1, bf16[1,128,1536]{2,1,0:T(8,128)(2,1)} %g_far.1), custom_call_target="tpu_custom_call" | custom-call | tf_op jit(solution)/shard_map/attention_grads/pallas_call | solution.py:562
  68.8 2.1 %results.1 = (bf16[1,128,1536]{2,1,0:T(8,128)(2,1)}, bf16[1,128,512]{2,1,0:T(8,128)(2,1)}, bf16[1,128,512]{2,1,0:T(8,128)(2,1)}) custom-call(bf16[8,3,64,128]{3,2,1,0:T(8,128)(2,1)} %get-tuple-element.5.dq_in, bf16[8,128,128]{2,1,0:T(8,128)(2,1)} %get-tuple-element.6.dkv_in), custom_call_target="tpu_custom_call" | custom-call | tf_op jit(solution)/shard_map/results/pallas_call | solution.py:620

commit v5 on v4

--- a/solution.py
+++ b/solution.py
@@ -451,8 +451,12 @@
         return 0
 
     def sweep(t, _):
-        next_block(1, final, turn(t - 1), turn(t))
-        hand_out(turn(t - 1))
+        before, b = turn(t - 1), turn(t)
+        weigh(1, final, b, 0)
+        gather(1, final, before, 1)
+        hand_out(before)
+        weigh(1, final, b, 1)
+        gather(1, final, b, 0)
         return tidy(t, 0)
 
     def late_sum(t, _):
@@ -471,8 +475,8 @@
     send_dq(1, final)
     middle = top + 1 - SUM_LAG
     start = max(0, top + 1 - REDUCE_LAG)
+    lax.fori_loop(middle, top + 1, late_sum, 0)
     lax.fori_loop(start, middle, late_reduce, 0)
-    lax.fori_loop(middle, top + 1, late_sum, 0)
     lax.fori_loop(middle, top + 1, late_reduce, 0)
 
     for h in range(kv_heads):

time: 71 us -> 70.3 us (level)
  no operation moved by 1% of the time
where the time goes in v5:
time: 70.3 us; the launch traced here: 70.1 us
  Pallas kernels  69.5 us (99%)
    pallas_call x1, Pallas kernels, per_device(): pl.pallas_call(functools.partial(kernel, kv_heads, resident), out_shape=(...  67.4 us
    pallas_call x1, Pallas kernels, per_device(): pl.pallas_call(results, out_shape=(jax.ShapeDtypeStruct(queries.shape, lo...  2.05 us

profile of v5, /device:TPU:0, one launch (start us, length us, event | category | flops | bytes accessed | tf_op | source)
XLA Modules:
  0.0 70.1 jit_solution(4720657658707836994)
XLA Ops:
  0.6 67.4 %attention_grads.1 = (bf16[8,3,64,128]{3,2,1,0:T(8,128)(2,1)}, bf16[8,128,128]{2,1,0:T(8,128)(2,1)}) custom-call(bf16[1,128,1536]{2,1,0:T(8,128)(2,1)} %q_far.1, bf16[1,128,512]{2,1,0:T(8,128)(2,1)} %k_far.1, bf16[1,128,512]{2,1,0:T(8,128)(2,1)} %v_far.1, bf16[1,128,1536]{2,1,0:T(8,128)(2,1)} %o_far.1, bf16[1,128,1536]{2,1,0:T(8,128)(2,1)} %g_far.1), custom_call_target="tpu_custom_call" | custom-call | tf_op jit(solution)/shard_map/attention_grads/pallas_call | solution.py:566
  68.1 2.1 %results.1 = (bf16[1,128,1536]{2,1,0:T(8,128)(2,1)}, bf16[1,128,512]{2,1,0:T(8,128)(2,1)}, bf16[1,128,512]{2,1,0:T(8,128)(2,1)}) custom-call(bf16[8,3,64,128]{3,2,1,0:T(8,128)(2,1)} %get-tuple-element.5.dq_in, bf16[8,128,128]{2,1,0:T(8,128)(2,1)} %get-tuple-element.6.dkv_in), custom_call_target="tpu_custom_call" | custom-call | tf_op jit(solution)/shard_map/results/pallas_call | solution.py:624
